TPU v7x, 32 devices: a whole 2x2x4 slice. The times are simulated.
32 devices in a mesh: seq: 8 (over y, x, core), head: 4 (over z).
Axes of the slice: x: 2, y: 2, z: 4, core: 2. Of those that a mesh axis runs over, the one named last changes fastest.
Arguments:
- values: bfloat16 [4096, 8192], P('seq', 'head'), may hold values from -6 to 6
- group_keys: bfloat16 [4096, 8, 128], P(('seq', 'head')), may hold values from -0.5 to 0.5
- group_queries: bfloat16 [4096, 8, 128], P(('seq', 'head')), may hold values from -0.16992188 to 0.16992188
- level_table: int32 [128, 20], P('head'), may hold values from 1 to 4
- window_index: int32 [1], replicated, may hold values from 0 to 15
- prior_states: bfloat16 [4, 128, 64, 128], P(None, 'head'), may hold values from -100 to 100
- cotangent: bfloat16 [4096, 8192], P('seq', 'head'), may hold values from -6 to 6
Outputs:
- mixer_out: bfloat16 [4096, 8192], P('seq', 'head')
- grad_values: bfloat16 [4096, 8192], P('seq', 'head')
- grad_keys: float32 [4096, 8, 128], P(('seq', 'head'))
- grad_queries: float32 [4096, 8, 128], P(('seq', 'head'))
- grad_prior: float32 [4, 128, 64, 128], P(None, 'head')
All inputs are finite; a program needn't handle non-finite values.
Results may differ from a plain program's by a relative error of at most 0.015.
Values may be sent and summed in bfloat16 or wider, within the bound.
No kernel may reach another device: no remote copies, remote signals or barrier semaphores. Data moves between devices by JAX's collectives and lax.ppermute only.
A program may use at most 128 MiB of HBM per device.

v0:
```python
import functools

import jax
import jax.numpy as jnp
from jax import lax
from jax.experimental import pallas as pl
from jax.experimental.pallas import tpu as pltpu
from jax.sharding import PartitionSpec as P


HEADS = 128
GROUPS = 8
BF = jnp.bfloat16
F32 = jnp.float32
SMEM = pl.BlockSpec(memory_space=pltpu.SMEM)
VMEM = pl.BlockSpec(memory_space=pltpu.VMEM)
PARAMS = pltpu.CompilerParams(vmem_limit_bytes=24 << 20)


def near_core(array):
    return pltpu.with_memory_space_constraint(array, pltpu.VMEM)


def swap_with(array, axis, mask):
    return lax.ppermute(array, axis, [(i, i ^ mask) for i in range(lax.axis_size(axis))])


def dot_nn(a, b):
    return lax.dot_general(a, b, (((1,), (0,)), ((), ())), preferred_element_type=F32)


def dot_nt(a, b):
    return lax.dot_general(a, b, (((1,), (1,)), ((), ())), preferred_element_type=F32)


def dot_tn(a, b):
    return lax.dot_general(a, b, (((0,), (0,)), ((), ())), preferred_element_type=F32)


def shaped(shape, dtype):
    return jax.ShapeDtypeStruct(shape, dtype)


def cost(flops, bytes_accessed):
    return pl.CostEstimate(flops=flops, transcendentals=0, bytes_accessed=bytes_accessed)


def weight(table_ref, head, level):
    return table_ref[head, level].astype(F32) * 2.0 ** (-max(level - 1, 0) / 2)


def log2(number):
    return number.bit_length() - 1


def prep_kernel(*refs, pieces):
    x_refs, outs, scratch = refs[:2], refs[2:-1], refs[-1]
    here = lax.axis_index("head")
    for n, x_ref in enumerate(x_refs):
        scratch[...] = jnp.swapaxes(x_ref[...].astype(F32), 0, 1)
        for r, out in enumerate(outs[n * pieces : (n + 1) * pieces]):
            take = out.shape[0]
            out[...] = scratch[pl.ds((here ^ r) * take, take)].astype(out.dtype)


def prep(keys, queries, pieces):
    rows, groups, state = keys.shape
    out = pl.pallas_call(
        functools.partial(prep_kernel, pieces=pieces),
        in_specs=[VMEM] * 2,
        out_specs=[VMEM] * (2 * pieces),
        out_shape=[pltpu.VMEM((groups // pieces, rows, state), BF)] * (2 * pieces),
        scratch_shapes=[pltpu.VMEM((groups, rows, state), F32)],
        compiler_params=PARAMS,
        cost_estimate=cost(10**6, 8 * keys.size),
        name="prep",
    )(keys, queries)
    return out[:pieces], out[pieces:]


def states_kernel(x_ref, *refs):
    parts, (o_ref, rows_ref) = refs[:-2], refs[-2:]
    if len(parts) == 1:
        rows_ref[...] = parts[0][...]
    else:
        here = lax.axis_index("head")
        size = parts[0].shape[1]
        for r, part in enumerate(parts):
            rows_ref[:, pl.ds(pl.multiple_of((here ^ r) * size, size), size), :] = part[...]
    groups = rows_ref.shape[0]
    width = x_ref.shape[1] // groups
    for g in range(groups):
        span = slice(g * width, (g + 1) * width)
        o_ref[span, :] = dot_tn(rows_ref[g], x_ref[:, span]).T.astype(o_ref.dtype)


def block_states(x, parts):
    tok, width = x.shape
    lg, _, state = parts[0].shape
    return pl.pallas_call(
        states_kernel,
        in_specs=[VMEM] * (1 + len(parts)),
        out_specs=[VMEM] * 2,
        out_shape=[pltpu.VMEM((width, state), BF), pltpu.VMEM((lg, tok, state), BF)],
        compiler_params=PARAMS,
        cost_estimate=cost(2 * tok * width * state, 2 * tok * width),
        name="states",
    )(x, *[near_core(part) for part in parts])


def spread_grid(base):
    rows = lax.broadcasted_iota(jnp.int32, (base, base), 0)
    cols = lax.broadcasted_iota(jnp.int32, (base, base), 1)
    return rows, cols, rows ^ cols


def factor_of(table_ref, head, spread, base):
    out = jnp.full((base, base), weight(table_ref, head, 0), F32)
    for level in range(1, log2(base) + 1):
        out = jnp.where(spread >= 1 << (level - 1), weight(table_ref, head, level), out)
    return out


def sides(base, head_dim):
    lane = lax.broadcasted_iota(jnp.int32, (base, 2 * head_dim), 1)
    return lane < head_dim, (lane < head_dim).astype(BF), (lane >= head_dim).astype(BF)


def blk(i, base, n=1):
    return pl.ds(i * base, n * base)


def pair_weights(table_ref, first_head, pairs, level, is_left):
    rows = [
        jnp.where(
            is_left,
            weight(table_ref, first_head + 2 * p, level),
            weight(table_ref, first_head + 2 * p + 1, level),
        )
        for p in range(pairs)
    ]
    return jnp.concatenate(rows, axis=1)


def gram_kernel(table_ref, v_ref, c_ref, g_ref, g_sc, *, base, head_dim, group, cols):
    tok = v_ref.shape[0]
    blocks = tok // base
    heads = cols // head_dim
    step = pl.program_id(0)
    at = group * pl.num_programs(0) + step
    first_head = at * heads
    first_col = pl.multiple_of(at * cols, cols)
    rows_i, cols_i, spread = spread_grid(base)
    is_left, left, right = sides(base, head_dim)

    @pl.when(step == 0)
    def _():
        g_sc[...] = jnp.zeros_like(g_sc)

    for pair in range(heads // 2):
        span = pl.ds(first_col + pair * 2 * head_dim, 2 * head_dim)
        f_a = factor_of(table_ref, first_head + 2 * pair, spread, base)
        f_b = factor_of(table_ref, first_head + 2 * pair + 1, spread, base)
        for i in range(blocks):
            v_i, c_i = v_ref[blk(i, base), span], c_ref[blk(i, base), span]
            raw = dot_nt(c_i, jnp.concatenate([v_i * left, v_i * right], axis=0))
            g_sc[blk(i, base), blk(i, base)] += f_a * raw[:, :base] + f_b * raw[:, base:]
    span = pl.ds(first_col, cols)
    for k in range(log2(blocks)):
        cw = pair_weights(table_ref, first_head, heads // 2, log2(base) + 1 + k, is_left[:1])
        for i in range(blocks):
            if i >> k & 1:
                there = blk((i >> k ^ 1) << k, base, 1 << k)
                scaled = (c_ref[blk(i, base), span].astype(F32) * cw).astype(BF)
                g_sc[blk(i, base), there] += dot_nt(scaled, v_ref[there, span])

    @pl.when(step == pl.num_programs(0) - 1)
    def _():
        for i in range(blocks):
            here = blk(i, base)
            g_sc[here, here] = jnp.where(rows_i >= cols_i, g_sc[here, here], 0.0)
        g_ref[...] = g_sc[...].astype(BF)


def gram(table, values, cotangent, group, groups, head_dim, cols):
    tok, width = values.shape
    base = min(128, tok)
    return pl.pallas_call(
        functools.partial(gram_kernel, base=base, head_dim=head_dim, group=group, cols=cols),
        grid=(width // groups // cols,),
        in_specs=[SMEM, VMEM, VMEM],
        out_specs=VMEM,
        out_shape=pltpu.VMEM((tok, tok), BF),
        scratch_shapes=[pltpu.VMEM((tok, tok), F32)],
        compiler_params=PARAMS,
        cost_estimate=cost(2 * tok * tok * width // groups, 4 * tok * width // groups),
        name="gram",
    )(table, values, cotangent)


def intra_kernel(table_ref, v_ref, c_ref, kg_rows, qg_rows, g_ref, *refs, base, head_dim, group, cols):
    mix_ref, dv_ref, qg_ref, kg_ref, s_sc, st_sc, sb_sc, stb_sc = refs[-8:]
    k_ref, q_ref = kg_rows.at[group], qg_rows.at[group]
    tok = v_ref.shape[0]
    blocks = tok // base
    heads = cols // head_dim
    step = pl.program_id(0)
    at = group * pl.num_programs(0) + step
    first_head = at * heads
    first_col = pl.multiple_of(at * cols, cols)
    rows_i, cols_i, spread = spread_grid(base)
    is_left, left, right = sides(base, head_dim)

    @pl.when(step == 0)
    def _():
        for i in range(blocks):
            here = blk(i, base)
            q_i, k_i = q_ref[here, :], k_ref[here, :]
            s_sc[here, :] = jnp.where(rows_i >= cols_i, dot_nt(q_i, k_i), 0.0)
            st_sc[here, :] = jnp.where(rows_i <= cols_i, dot_nt(k_i, q_i), 0.0)
            above = blk(0, base, i)
            rest = blk(i + 1, base, blocks - 1 - i)
            if i > 0:
                sb_sc[here, above] = dot_nt(q_i, k_ref[above, :]).astype(BF)
            if i < blocks - 1:
                stb_sc[here, rest] = dot_nt(k_i, q_ref[rest, :]).astype(BF)
            until = blk(0, base, i + 1)
            below = blk(i, base, blocks - i)
            qg_ref[here, :] = dot_nn(g_ref[here, until], k_ref[until, :])
            kg_ref[here, :] = dot_tn(g_ref[below, here], q_ref[below, :])

    mix = [[] for _ in range(blocks)]
    dv = [[] for _ in range(blocks)]
    for pair in range(heads // 2):
        span = pl.ds(first_col + pair * 2 * head_dim, 2 * head_dim)
        f_a = factor_of(table_ref, first_head + 2 * pair, spread, base)
        f_b = factor_of(table_ref, first_head + 2 * pair + 1, spread, base)
        for i in range(blocks):
            here = blk(i, base)
            for f_ref, x_ref, out in ((s_sc, v_ref, mix), (st_sc, c_ref, dv)):
                s_i, x_i = f_ref[here, :], x_ref[here, span]
                w_cat = jnp.concatenate([(f_a * s_i).astype(BF), (f_b * s_i).astype(BF)], axis=1)
                stacked = jnp.concatenate([x_i * left, x_i * right], axis=0)
                out[i].append(dot_nn(w_cat, stacked))
    scales = [
        pair_weights(table_ref, first_head, heads // 2, log2(base) + 1 + k, is_left[:1])
        for k in range(log2(blocks))
    ]
    span = pl.ds(first_col, cols)
    for i in range(blocks):
        here = blk(i, base)
        mix_i = jnp.concatenate(mix[i], axis=1)
        dv_i = jnp.concatenate(dv[i], axis=1)
        for k, cw in enumerate(scales):
            there = blk((i >> k ^ 1) << k, base, 1 << k)
            if i >> k & 1:
                mix_i += dot_nn(sb_sc[here, there], v_ref[there, span]) * cw
            else:
                dv_i += dot_nn(stb_sc[here, there], c_ref[there, span]) * cw
        mix_ref[here, span] = mix_i.astype(mix_ref.dtype)
        dv_ref[here, span] = dv_i.astype(dv_ref.dtype)


def intra(table, values, cotangent, keys, queries, grams, before, group, head_dim, cols):
    tok, width = values.shape
    groups, _, state = keys.shape
    base = min(128, tok)
    return pl.pallas_call(
        functools.partial(intra_kernel, base=base, head_dim=head_dim, group=group, cols=cols),
        grid=(width // groups // cols,),
        in_specs=[SMEM] + [VMEM] * (5 + len(before)),
        out_specs=[VMEM] * 4,
        out_shape=[pltpu.VMEM((tok, width), BF)] * 2 + [pltpu.VMEM((tok, state), F32)] * 2,
        input_output_aliases={6 + n: n for n in range(len(before))},
        scratch_shapes=[pltpu.VMEM((tok, base), F32)] * 2 + [pltpu.VMEM((tok, tok), BF)] * 2,
        compiler_params=PARAMS,
        cost_estimate=cost(4 * tok * tok * width // groups, 8 * tok * width // groups),
        name="intra",
    )(table, values, cotangent, keys, queries, grams, *before)


def near_kernel(table_ref, window_ref, p_ref, *refs, level, gate, head_dim, prior_level):
    o_ref = refs[-1]
    priors = refs[0] if len(refs) > 1 else None
    heads = o_ref.shape[0] // head_dim
    on = (lax.axis_index("seq") & 1 == gate).astype(F32)
    for h in range(heads):
        rows = blk(h, head_dim)
        out = p_ref[rows, :].astype(F32) * (weight(table_ref, h, level) * on)
        if priors is not None:
            for k in range(priors.shape[0]):
                bit = (window_ref[0] >> k & 1).astype(F32)
                out += priors[k, rows, :].astype(F32) * (weight(table_ref, h, prior_level + k) * bit)
        o_ref[rows, :] = out


def near(table, window, partner, priors, level, gate, head_dim, prior_level):
    width, state = partner.shape
    ins = [near_core(x) for x in (partner, priors) if x is not None]
    return pl.pallas_call(
        functools.partial(
            near_kernel, level=level, gate=gate, head_dim=head_dim, prior_level=prior_level
        ),
        in_specs=[SMEM, SMEM] + [VMEM] * len(ins),
        out_specs=VMEM,
        out_shape=pltpu.VMEM((width, state), F32),
        compiler_params=PARAMS,
        cost_estimate=cost(10 * width * state, 8 * width * state),
        name="near",
    )(table, window, *ins)


def combine_kernel(a_ref, b_ref, o_ref):
    half = o_ref.shape[0]
    rows = pl.ds(0, half)
    if a_ref.shape[0] > half:
        rows = pl.ds(pl.multiple_of((lax.axis_index("seq") & 1) * half, half), half)
    total = a_ref[rows, :].astype(F32) + b_ref[rows, :].astype(F32)
    o_ref[...] = total.astype(o_ref.dtype)


def combine(a, b, half):
    return pl.pallas_call(
        combine_kernel,
        in_specs=[VMEM] * 2,
        out_specs=VMEM,
        out_shape=pltpu.VMEM((half, a.shape[1]), BF),
        compiler_params=PARAMS,
        cost_estimate=cost(a.size, 4 * a.size),
        name="combine",
    )(near_core(a), near_core(b))


def far_kernel(table_ref, *refs, level, gate, head_dim, with_total):
    o_ref = refs[-1]
    partners = refs[:-2] if with_total else refs[:-1]
    half = partners[0].shape[0]
    heads = half // head_dim
    seq = lax.axis_index("seq")
    first = (seq & 1) * heads
    ons = [(seq >> (k + 1) & 1 == gate).astype(F32) for k in range(len(partners))]
    for h in range(heads):
        rows = blk(h, head_dim)
        out = None
        for k, p_ref in enumerate(partners):
            term = p_ref[rows, :].astype(F32) * (
                weight(table_ref, first + h, level + k) * ons[k]
            )
            out = term if out is None else out + term
        o_ref[rows, :] = out.astype(o_ref.dtype)
    if with_total:
        total = refs[-2][...].astype(F32) + partners[-1][...].astype(F32)
        o_ref[pl.ds(half, half), :] = total.astype(o_ref.dtype)


def far(table, partners, before, level, gate, head_dim):
    half, state = partners[0].shape
    extra = [] if before is None else [before]
    return pl.pallas_call(
        functools.partial(
            far_kernel, level=level, gate=gate, head_dim=head_dim, with_total=bool(extra)
        ),
        in_specs=[SMEM] + [VMEM] * (len(partners) + len(extra)),
        out_specs=VMEM,
        out_shape=pltpu.VMEM((half * (1 + len(extra)), state), BF),
        compiler_params=PARAMS,
        cost_estimate=cost(10 * half * state, 8 * half * state),
        name="far",
    )(table, *[near_core(x) for x in partners + extra])


def finish_kernel(
    part_ref, r_ref, near_ref, mine_ref, other_ref, x_ref, *refs, pieces, halves, cols
):
    groups = r_ref.shape[0]
    g_refs, o_ref, outs, acc = refs[:groups], refs[groups], refs[groups + 1 : -1], refs[-1]
    group, step = pl.program_id(0), pl.program_id(1)
    at = group * pl.num_programs(1) + step
    is_mine = at // halves == lax.axis_index("seq") & 1
    span = pl.ds(pl.multiple_of(at * cols, cols), cols)
    half = pl.ds(pl.multiple_of(at % halves * cols, cols), cols)
    flow = near_ref[span, :] + jnp.where(is_mine, mine_ref[half, :], other_ref[half, :]).astype(F32)
    flow = flow.astype(BF)
    o_ref[...] = (part_ref[:, span].astype(F32) + dot_nt(r_ref[group], flow)).astype(o_ref.dtype)
    for g in range(groups):

        @pl.when((step == 0) & (group == g))
        def _():
            acc[...] = g_refs[g][...]

    acc[...] += dot_nn(x_ref[:, span], flow)

    @pl.when(step == pl.num_programs(1) - 1)
    def _():
        if pieces == 1:
            outs[0][group] = acc[...].astype(BF)
        else:
            here = lax.axis_index("head")
            size = outs[0].shape[1]
            for r, out in enumerate(outs):
                rows = pl.ds(pl.multiple_of((here ^ r) * size, size), size)
                out[group] = acc[rows, :].astype(BF)


def finish(part, rows, near_flow, mine, other, x, grads, cols, pieces):
    tok, width = part.shape
    groups, _, state = rows.shape
    steps = width // groups // cols
    piece = (groups, tok // pieces, state)
    return pl.pallas_call(
        functools.partial(finish_kernel, pieces=pieces, halves=width // cols // 2, cols=cols),
        grid=(groups, steps),
        in_specs=[VMEM] * (6 + groups),
        out_specs=[pl.BlockSpec((tok, cols), lambda g, j: (0, g * steps + j))] + [VMEM] * pieces,
        out_shape=[shaped((tok, width), BF)] + [pltpu.VMEM(piece, BF)] * pieces,
        scratch_shapes=[pltpu.VMEM((tok, state), F32)],
        compiler_params=PARAMS,
        cost_estimate=cost(4 * tok * width * state, 6 * tok * width),
        name="finish",
    )(part, rows, near_flow, near_core(mine), near_core(other), x, *grads)


def gather_kernel(*refs):
    parts, o_ref, scratch = refs[:-2], refs[-2], refs[-1]
    here = lax.axis_index("head")
    take = parts[0].shape[0]
    for r, part in enumerate(parts):
        scratch[pl.ds((here ^ r) * take, take)] = part[...].astype(F32)
    o_ref[...] = jnp.swapaxes(scratch[...], 0, 1)


def gather(parts):
    take, rows, state = parts[0].shape
    groups = take * len(parts)
    return pl.pallas_call(
        gather_kernel,
        in_specs=[VMEM] * len(parts),
        out_specs=pl.BlockSpec((rows, groups, state), lambda: (0, 0, 0)),
        out_shape=shaped((rows, groups, state), F32),
        scratch_shapes=[pltpu.VMEM((groups, rows, state), F32)],
        compiler_params=PARAMS,
        cost_estimate=cost(10**6, 6 * groups * rows * state),
        name="gather",
    )(*[near_core(part) for part in parts])


def prior_kernel(table_ref, window_ref, mine_ref, other_ref, o_ref, *, head_dim, level, halves):
    at = pl.program_id(0)
    size = o_ref.shape[1]
    heads = size // head_dim
    is_mine = at // halves == lax.axis_index("seq") & 1
    rows = pl.ds(pl.multiple_of((halves + at % halves) * size, size), size)
    total = jnp.where(is_mine, mine_ref[rows, :], other_ref[rows, :]).astype(F32)
    for h in range(heads):
        rows = slice(h * head_dim, (h + 1) * head_dim)
        for k in range(o_ref.shape[0]):
            bit = (window_ref[0] >> k & 1).astype(F32)
            o_ref[k, rows, :] = total[rows] * (weight(table_ref, at * heads + h, level + k) * bit)


def prior_grad(table, window, mine, other, count, level, head_dim, steps):
    half = mine.shape[0] // 2
    state = mine.shape[1]
    halves = steps // 2
    rows = half // halves
    return pl.pallas_call(
        functools.partial(prior_kernel, head_dim=head_dim, level=level, halves=halves),
        grid=(steps,),
        in_specs=[SMEM, SMEM, VMEM, VMEM],
        out_specs=pl.BlockSpec((count, rows, state), lambda i: (0, i, 0)),
        out_shape=shaped((count, 2 * half, state), F32),
        compiler_params=PARAMS,
        cost_estimate=cost(2 * count * half * state, 8 * count * half * state),
        name="prior_grad",
    )(table, window, near_core(mine), near_core(other))


def mixer(
    values, group_keys, group_queries, level_table, window_index, prior_states, cotangent
):
    seq_count = lax.axis_size("seq")
    head_count = lax.axis_size("head")
    tok_rows = values.shape[0]
    heads_here = level_table.shape[0]
    head_dim = values.shape[1] // heads_here
    state_dim = group_keys.shape[2]
    group_count = group_keys.shape[1]
    prior_count = prior_states.shape[0]
    per_group = HEADS // GROUPS
    repeats = max(1, per_group // heads_here)
    local_groups = max(1, heads_here // per_group)
    heads_local = heads_here // local_groups
    log_rows = log2(tok_rows)
    log_seq = log2(seq_count)
    log_window = log_rows + log_seq
    width = heads_here * head_dim
    half = width // 2
    pieces = head_count if head_count <= 4 and repeats == 1 else 1
    cols_in = min(4, heads_local) * head_dim
    cols = min(8, heads_here // 2) * head_dim

    def scattered(own, *sent):
        out = [own]
        for r, part in enumerate(sent):
            out.append(swap_with(part, "head", r + 1))
        return out

    def rows_of(x):
        wide = jnp.repeat(x, repeats, axis=1).swapaxes(0, 1)
        wide = wide.reshape(head_count, local_groups, -1, state_dim)
        wide = lax.all_to_all(wide, "head", split_axis=0, concat_axis=0)
        return [wide.swapaxes(0, 1).reshape(local_groups, tok_rows, state_dim)]

    if pieces == 1:
        key_parts, query_parts = rows_of(group_keys), rows_of(group_queries)
    else:
        key_parts, query_parts = prep(group_keys, group_queries, pieces)
        key_parts = scattered(*key_parts)
        query_parts = scattered(*query_parts)
    values, cotangent = near_core(values), near_core(cotangent)
    grams = []
    for g in range(local_groups):
        grams.append(
            gram(level_table, values, cotangent, g, local_groups, head_dim, cols_in)
        )

    def exchange(own, gate, priors):
        partner = swap_with(own, "seq", 1)
        near_flow = near(
            level_table, window_index, partner, priors, 1 + log_rows, gate, head_dim,
            1 + log_window,
        )
        total = combine(own, partner, half)
        partners = []
        for bit in range(1, log_seq):
            partners.append(swap_with(total, "seq", 1 << bit))
            if bit < log_seq - 1:
                total = combine(total, partners[-1], half)
        before = None if priors is not None else total
        mine = far(level_table, partners, before, 2 + log_rows, gate, head_dim)
        other = swap_with(mine, "seq", 1)
        return near_flow, mine, other

    states, key_rows = block_states(values, key_parts)
    priors = prior_states.reshape(prior_count, width, state_dim)
    in_near, in_mine, in_other = exchange(states, 1, priors)
    adjoints, query_rows = block_states(cotangent, query_parts)
    out_near, out_mine, out_other = exchange(adjoints, 0, None)
    parts, query_grads, key_grads = [], [], []
    for g in range(local_groups):
        *parts, query_grad, key_grad = intra(
            level_table, values, cotangent, key_rows, query_rows, grams[g], parts, g,
            head_dim, cols_in,
        )
        query_grads.append(query_grad)
        key_grads.append(key_grad)
    mix_part, dv_part = parts

    def back(parts):
        if pieces == 1:
            part = parts[0].reshape(local_groups, head_count, -1, state_dim).swapaxes(0, 1)
            part = lax.all_to_all(part, "head", split_axis=0, concat_axis=0).astype(F32)
            part = part.reshape(group_count, repeats, -1, state_dim).sum(axis=1)
            return part.swapaxes(0, 1)
        parts = scattered(*parts)
        return gather(parts)

    mixer_out, *query_parts = finish(
        mix_part, query_rows, in_near, in_mine, in_other, cotangent, query_grads, cols, pieces
    )
    grad_queries = back(query_parts)
    grad_values, *key_parts = finish(
        dv_part, key_rows, out_near, out_mine, out_other, values, key_grads, cols, pieces
    )
    grad_keys = back(key_parts)
    grad_prior = prior_grad(
        level_table, window_index, out_mine, out_other, prior_count, 1 + log_window, head_dim,
        width // cols,
    )
    return (mixer_out, grad_values, grad_keys, grad_queries, grad_prior.reshape(prior_states.shape))


def solution(mesh):
    placed = (
        P("seq", "head"),
        P(("seq", "head"), None, None),
        P(("seq", "head"), None, None),
        P("head", None),
        P(),
        P(None, "head", None, None),
        P("seq", "head"),
    )
    return jax.shard_map(
        mixer,
        mesh=mesh,
        in_specs=placed,
        out_specs=(
            P("seq", "head"),
            P("seq", "head"),
            P(("seq", "head"), None, None),
            P(("seq", "head"), None, None),
            P(None, "head", None, None),
        ),
        check_vma=False,
    )
```

profile of v0, /device:TPU:0, one launch (start us, length us, event | category | flops | bytes accessed | tf_op | source)
XLA Modules:
  0.0 92.1 jit_solution(6295538676543995017)
XLA Ops:
  2.9 3.1 %collective-permute-start.3 = (bf16[2,128,128]{2,1,0:T(8,128)(2,1)S(1)}, bf16[2,128,128]{2,1,0:T(8,128)(2,1)S(1)}, u32[]{:S(2)}, u32[]{:S(2)}) collective-permute-start(bf16[2,128,128]{2,1,0:T(8,128)(2,1)S(1)} %get-tuple-element.41), channel_id=1, source_target_pairs={{0,1},{1,0},{2,3},{3,2},{4,5},{5,4},{6,7},{7,6},{8,9},{9,8},{10,11... | collective-permute-start | bytes 196616 | tf_op jit(solution)/shard_map/ppermute | solution.py:25
  6.0 2.6 %collective-permute-start.4 = (bf16[2,128,128]{2,1,0:T(8,128)(2,1)S(1)}, bf16[2,128,128]{2,1,0:T(8,128)(2,1)S(1)}, u32[]{:S(2)}, u32[]{:S(2)}) collective-permute-start(bf16[2,128,128]{2,1,0:T(8,128)(2,1)S(1)} %get-tuple-element.42), channel_id=1, source_target_pairs={{0,2},{1,3},{2,0},{3,1},{4,6},{5,7},{6,4},{7,5},{8,10},{9,11},{10,... | collective-permute-start | bytes 196616 | tf_op jit(solution)/shard_map/ppermute | solution.py:25
  8.6 4.7 %collective-permute-done.4.refs_2_ = bf16[2,128,128]{2,1,0:T(8,128)(2,1)S(1)} collective-permute-done((bf16[2,128,128]{2,1,0:T(8,128)(2,1)S(1)}, bf16[2,128,128]{2,1,0:T(8,128)(2,1)S(1)}, u32[]{:S(2)}, u32[]{:S(2)}) %collective-permute-start.4) | collective-permute-done | bytes 65568 | tf_op jit(solution)/shard_map/ppermute | solution.py:25
  13.2 1.4 %collective-permute-done.5.refs_3_ = bf16[2,128,128]{2,1,0:T(8,128)(2,1)S(1)} collective-permute-done((bf16[2,128,128]{2,1,0:T(8,128)(2,1)S(1)}, bf16[2,128,128]{2,1,0:T(8,128)(2,1)S(1)}, u32[]{:S(2)}, u32[]{:S(2)}) %collective-permute-start.5) | collective-permute-done | bytes 65568 | tf_op jit(solution)/shard_map/ppermute | solution.py:25
  14.7 1.6 %copy-done = bf16[512,2048]{1,0:T(8,128)(2,1)S(1)} copy-done((bf16[512,2048]{1,0:T(8,128)(2,1)S(1)}, bf16[512,2048]{1,0:T(8,128)(2,1)}, u32[]{:S(2)}) %copy-start) | copy-done | bytes 2097176
  17.0 2.3 %collective-permute-start.1 = (bf16[2,128,128]{2,1,0:T(8,128)(2,1)S(1)}, bf16[2,128,128]{2,1,0:T(8,128)(2,1)S(1)}, u32[]{:S(2)}, u32[]{:S(2)}) collective-permute-start(bf16[2,128,128]{2,1,0:T(8,128)(2,1)S(1)} %get-tuple-element.37), channel_id=1, source_target_pairs={{0,2},{1,3},{2,0},{3,1},{4,6},{5,7},{6,4},{7,5},{8,10},{9,11},{10,... | collective-permute-start | bytes 196616 | tf_op jit(solution)/shard_map/ppermute | solution.py:25
  19.3 2.0 %collective-permute-start.2 = (bf16[2,128,128]{2,1,0:T(8,128)(2,1)S(1)}, bf16[2,128,128]{2,1,0:T(8,128)(2,1)S(1)}, u32[]{:S(2)}, u32[]{:S(2)}) collective-permute-start(bf16[2,128,128]{2,1,0:T(8,128)(2,1)S(1)} %get-tuple-element.38), channel_id=1, source_target_pairs={{0,3},{1,2},{2,1},{3,0},{4,7},{5,6},{6,5},{7,4},{8,11},{9,10},{10,... | collective-permute-start | bytes 196616 | tf_op jit(solution)/shard_map/ppermute | solution.py:25
  21.4 1.4 %collective-permute-done.refs_1_ = bf16[2,128,128]{2,1,0:T(8,128)(2,1)S(1)} collective-permute-done((bf16[2,128,128]{2,1,0:T(8,128)(2,1)S(1)}, bf16[2,128,128]{2,1,0:T(8,128)(2,1)S(1)}, u32[]{:S(2)}, u32[]{:S(2)}) %collective-permute-start) | collective-permute-done | bytes 65568 | tf_op jit(solution)/shard_map/ppermute | solution.py:25
  22.8 2.6 %collective-permute-done.2.refs_3_ = bf16[2,128,128]{2,1,0:T(8,128)(2,1)S(1)} collective-permute-done((bf16[2,128,128]{2,1,0:T(8,128)(2,1)S(1)}, bf16[2,128,128]{2,1,0:T(8,128)(2,1)S(1)}, u32[]{:S(2)}, u32[]{:S(2)}) %collective-permute-start.2) | collective-permute-done | bytes 65568 | tf_op jit(solution)/shard_map/ppermute | solution.py:25
  26.2 1.6 %collective-permute-start.11 = (bf16[1024,128]{1,0:T(8,128)(2,1)S(1)}, bf16[1024,128]{1,0:T(8,128)(2,1)S(1)}, u32[]{:S(2)}, u32[]{:S(2)}) collective-permute-start(bf16[1024,128]{1,0:T(8,128)(2,1)S(1)} %combine.6.a_ref), channel_id=1, source_target_pairs={{0,8},{4,12},{8,0},{12,4},{16,24},{20,28},{24,16},{28,20},{1,9},{5... | collective-permute-start | bytes 786440 | tf_op jit(solution)/shard_map/ppermute | solution.py:25
  28.8 1.5 %collective-permute-start.7 = (bf16[1024,128]{1,0:T(8,128)(2,1)S(1)}, bf16[1024,128]{1,0:T(8,128)(2,1)S(1)}, u32[]{:S(2)}, u32[]{:S(2)}) collective-permute-start(bf16[1024,128]{1,0:T(8,128)(2,1)S(1)} %combine.4.a_ref), channel_id=1, source_target_pairs={{0,8},{4,12},{8,0},{12,4},{16,24},{20,28},{24,16},{28,20},{1,9},{5... | collective-permute-start | bytes 786440 | tf_op jit(solution)/shard_map/ppermute | solution.py:25
  30.3 5.1 %collective-permute-done.11.b_ref.refs_0_ = bf16[1024,128]{1,0:T(8,128)(2,1)S(1)} collective-permute-done((bf16[1024,128]{1,0:T(8,128)(2,1)S(1)}, bf16[1024,128]{1,0:T(8,128)(2,1)S(1)}, u32[]{:S(2)}, u32[]{:S(2)}) %collective-permute-start.11) | collective-permute-done | bytes 262176 | tf_op jit(solution)/shard_map/ppermute | solution.py:25
  36.2 1.5 %collective-permute-start.12 = (bf16[1024,128]{1,0:T(8,128)(2,1)}, bf16[1024,128]{1,0:T(8,128)(2,1)}, u32[]{:S(2)}, u32[]{:S(2)}) collective-permute-start(bf16[1024,128]{1,0:T(8,128)(2,1)} %combine.7.refs_2_), channel_id=1, source_target_pairs={{0,16},{4,20},{8,24},{12,28},{16,0},{20,4},{24,8},{28,12},{1,17},{... | collective-permute-start | bytes 786440 | tf_op jit(solution)/shard_map/ppermute | solution.py:25
  37.7 2.8 %collective-permute-done.7.b_ref.refs_0_ = bf16[1024,128]{1,0:T(8,128)(2,1)S(1)} collective-permute-done((bf16[1024,128]{1,0:T(8,128)(2,1)S(1)}, bf16[1024,128]{1,0:T(8,128)(2,1)S(1)}, u32[]{:S(2)}, u32[]{:S(2)}) %collective-permute-start.7) | collective-permute-done | bytes 262176 | tf_op jit(solution)/shard_map/ppermute | solution.py:25
  41.3 1.5 %collective-permute-start.8 = (bf16[1024,128]{1,0:T(8,128)(2,1)}, bf16[1024,128]{1,0:T(8,128)(2,1)}, u32[]{:S(2)}, u32[]{:S(2)}) collective-permute-start(bf16[1024,128]{1,0:T(8,128)(2,1)} %combine.5), channel_id=1, source_target_pairs={{0,16},{4,20},{8,24},{12,28},{16,0},{20,4},{24,8},{28,12},{1,17},{... | collective-permute-start | bytes 786440 | tf_op jit(solution)/shard_map/ppermute | solution.py:25
  44.8 1.2 %far.3.mine_ref = bf16[2048,128]{1,0:T(8,128)(2,1)S(1)} custom-call(s32[32,20]{1,0:T(8,128)S(1)} %copy.17.table_ref, bf16[1024,128]{1,0:T(8,128)(2,1)S(1)} %copy-done.9, bf16[1024,128]{1,0:T(8,128)(2,1)} %collective-permute-done.12.refs_1_, bf16[1024,128]{1,0:T(8,128)(2,1)} %combine.7.refs_2_), custom_call_target="tpu_custom_call" | custom-call | flops 1310720 | bytes 1048576 | tf_op jit(solution)/shard_map/far/pallas_call | solution.py:359
  46.1 3.4 %collective-permute-done.8.refs_1_ = bf16[1024,128]{1,0:T(8,128)(2,1)} collective-permute-done((bf16[1024,128]{1,0:T(8,128)(2,1)}, bf16[1024,128]{1,0:T(8,128)(2,1)}, u32[]{:S(2)}, u32[]{:S(2)}) %collective-permute-start.8) | collective-permute-done | bytes 262176 | tf_op jit(solution)/shard_map/ppermute | solution.py:25
  49.5 1.1 %far.2.mine_ref = bf16[1024,128]{1,0:T(8,128)(2,1)S(1)} custom-call(s32[32,20]{1,0:T(8,128)S(1)} %copy.17.table_ref, bf16[1024,128]{1,0:T(8,128)(2,1)S(1)} %collective-permute-done.7.b_ref.refs_0_, bf16[1024,128]{1,0:T(8,128)(2,1)} %collective-permute-done.8.refs_1_), custom_call_target="tpu_custom_call" | custom-call | flops 1310720 | bytes 1048576 | tf_op jit(solution)/shard_map/far/pallas_call | solution.py:359
  50.7 1.6 %copy-done.3 = bf16[512,2048]{1,0:T(8,128)(2,1)S(1)} copy-done((bf16[512,2048]{1,0:T(8,128)(2,1)S(1)}, bf16[512,2048]{1,0:T(8,128)(2,1)}, u32[]{:S(2)}) %copy-start.3) | copy-done | bytes 2097176
  52.3 3.2 %gram.2.g_ref = bf16[512,512]{1,0:T(8,128)(2,1)S(1)} custom-call(s32[32,20]{1,0:T(8,128)S(1)} %copy.17.table_ref, bf16[512,2048]{1,0:T(8,128)(2,1)S(1)} %copy-done.3, bf16[512,2048]{1,0:T(8,128)(2,1)S(1)} %copy-done.1), custom_call_target="tpu_custom_call" | custom-call | flops 536870912 | bytes 2097152 | tf_op jit(solution)/shard_map/gram/pallas_call | solution.py:188
  56.1 3.2 %gram.3.g_ref = bf16[512,512]{1,0:T(8,128)(2,1)S(1)} custom-call(s32[32,20]{1,0:T(8,128)S(1)} %copy.17.table_ref, bf16[512,2048]{1,0:T(8,128)(2,1)S(1)} %copy-done.3, bf16[512,2048]{1,0:T(8,128)(2,1)S(1)} %copy-done.1), custom_call_target="tpu_custom_call" | custom-call | flops 536870912 | bytes 2097152 | tf_op jit(solution)/shard_map/gram/pallas_call | solution.py:188
  59.3 4.3 %intra.2 = (bf16[512,2048]{1,0:T(8,128)(2,1)S(1)}, bf16[512,2048]{1,0:T(8,128)(2,1)S(1)}, f32[512,128]{1,0:T(8,128)S(1)}, f32[512,128]{1,0:T(8,128)S(1)}) custom-call(s32[32,20]{1,0:T(8,128)S(1)} %copy.17.table_ref, bf16[512,2048]{1,0:T(8,128)(2,1)S(1)} %copy-done.3, bf16[512,2048]{1,0:T(8,128)(2,1)S(1)} %copy-done.1, ...), custom_call_target="tpu_custom_call" | custom-call | flops 1073741824 | bytes 4194304 | tf_op jit(solution)/shard_map/intra/pallas_call | solution.py:268
  63.6 4.2 %intra.3 = (bf16[512,2048]{1,0:T(8,128)(2,1)S(1)}, bf16[512,2048]{1,0:T(8,128)(2,1)S(1)}, f32[512,128]{1,0:T(8,128)S(1)}, f32[512,128]{1,0:T(8,128)S(1)}) custom-call(s32[32,20]{1,0:T(8,128)S(1)} %copy.17.table_ref, bf16[512,2048]{1,0:T(8,128)(2,1)S(1)} %copy-done.3, bf16[512,2048]{1,0:T(8,128)(2,1)S(1)} %copy-done.1, ...), custom_call_target="tpu_custom_call", output_to_operand_aliasing={{0}: (6, {}), {1}: (7, {})} | custom-call | flops 1073741824 | bytes 4194304 | tf_op jit(solution)/shard_map/intra/pallas_call | solution.py:268
  67.9 1.3 %near.2.near_ref = f32[2048,128]{1,0:T(8,128)S(1)} custom-call(s32[32,20]{1,0:T(8,128)S(1)} %copy.17.table_ref, s32[1]{0:T(128)S(6)} %copy.25.window_ref, bf16[2048,128]{1,0:T(8,128)(2,1)S(1)} %copy-done.7, bf16[4,2048,128]{2,1,0:T(8,128)(2,1)S(1)} %bitcast.2), custom_call_target="tpu_custom_call" | custom-call | flops 2621440 | bytes 2097152 | tf_op jit(solution)/shard_map/near/pallas_call | solution.py:300
  69.2 3.5 %finish.2 = (bf16[512,2048]{1,0:T(8,128)(2,1)}, bf16[2,128,128]{2,1,0:T(8,128)(2,1)S(1)}, bf16[2,128,128]{2,1,0:T(8,128)(2,1)S(1)}, bf16[2,128,128]{2,1,0:T(8,128)(2,1)S(1)}, bf16[2,128,128]{2,1,0:T(8,128)(2,1)S(1)}) custom-call(bf16[512,2048]{1,0:T(8,128)(2,1)S(1)} %get-tuple-element.47.part_ref, bf16[2,512,128]{2,1,0:T(8,128)(2,1)S(1)} %get-tuple-element.44.qg_rows.r_ref, ...), custom_call_target="tpu_custom_call" | custom-call | flops 536870912 | bytes 6291456 | tf_op jit(solution)/shard_map/finish/pallas_call | solution.py:410
  72.8 1.7 %collective-permute-start.17 = (bf16[2,128,128]{2,1,0:T(8,128)(2,1)S(1)}, bf16[2,128,128]{2,1,0:T(8,128)(2,1)S(1)}, u32[]{:S(2)}, u32[]{:S(2)}) collective-permute-start(bf16[2,128,128]{2,1,0:T(8,128)(2,1)S(1)} %get-tuple-element.62), channel_id=1, source_target_pairs={{0,1},{1,0},{2,3},{3,2},{4,5},{5,4},{6,7},{7,6},{8,9},{9,8},{10,11... | collective-permute-start | bytes 196616 | tf_op jit(solution)/shard_map/ppermute | solution.py:25
  75.4 1.7 %collective-permute-start.18 = (bf16[2,128,128]{2,1,0:T(8,128)(2,1)S(1)}, bf16[2,128,128]{2,1,0:T(8,128)(2,1)S(1)}, u32[]{:S(2)}, u32[]{:S(2)}) collective-permute-start(bf16[2,128,128]{2,1,0:T(8,128)(2,1)S(1)} %get-tuple-element.63), channel_id=1, source_target_pairs={{0,2},{1,3},{2,0},{3,1},{4,6},{5,7},{6,4},{7,5},{8,10},{9,11},{10,... | collective-permute-start | bytes 196616 | tf_op jit(solution)/shard_map/ppermute | solution.py:25
  77.1 1.2 %collective-permute-start.19 = (bf16[2,128,128]{2,1,0:T(8,128)(2,1)S(1)}, bf16[2,128,128]{2,1,0:T(8,128)(2,1)S(1)}, u32[]{:S(2)}, u32[]{:S(2)}) collective-permute-start(bf16[2,128,128]{2,1,0:T(8,128)(2,1)S(1)} %get-tuple-element.64), channel_id=1, source_target_pairs={{0,3},{1,2},{2,1},{3,0},{4,7},{5,6},{6,5},{7,4},{8,11},{9,10},{10,... | collective-permute-start | bytes 196616 | tf_op jit(solution)/shard_map/ppermute | solution.py:25
  78.3 3.5 %finish.3 = (bf16[512,2048]{1,0:T(8,128)(2,1)}, bf16[2,128,128]{2,1,0:T(8,128)(2,1)S(1)}, bf16[2,128,128]{2,1,0:T(8,128)(2,1)S(1)}, bf16[2,128,128]{2,1,0:T(8,128)(2,1)S(1)}, bf16[2,128,128]{2,1,0:T(8,128)(2,1)S(1)}) custom-call(bf16[512,2048]{1,0:T(8,128)(2,1)S(1)} %get-tuple-element.52.part_ref, bf16[2,512,128]{2,1,0:T(8,128)(2,1)S(1)} %get-tuple-element.39.kg_rows.r_ref, ...), custom_call_target="tpu_custom_call" | custom-call | flops 536870912 | bytes 6291456 | tf_op jit(solution)/shard_map/finish/pallas_call | solution.py:410
  82.4 2.5 %collective-permute-start.15 = (bf16[2,128,128]{2,1,0:T(8,128)(2,1)S(1)}, bf16[2,128,128]{2,1,0:T(8,128)(2,1)S(1)}, u32[]{:S(2)}, u32[]{:S(2)}) collective-permute-start(bf16[2,128,128]{2,1,0:T(8,128)(2,1)S(1)} %get-tuple-element.59), channel_id=1, source_target_pairs={{0,2},{1,3},{2,0},{3,1},{4,6},{5,7},{6,4},{7,5},{8,10},{9,11},{10,... | collective-permute-start | bytes 196616 | tf_op jit(solution)/shard_map/ppermute | solution.py:25
  84.9 1.2 %collective-permute-start.16 = (bf16[2,128,128]{2,1,0:T(8,128)(2,1)S(1)}, bf16[2,128,128]{2,1,0:T(8,128)(2,1)S(1)}, u32[]{:S(2)}, u32[]{:S(2)}) collective-permute-start(bf16[2,128,128]{2,1,0:T(8,128)(2,1)S(1)} %get-tuple-element.60), channel_id=1, source_target_pairs={{0,3},{1,2},{2,1},{3,0},{4,7},{5,6},{6,5},{7,4},{8,11},{9,10},{10,... | collective-permute-start | bytes 196616 | tf_op jit(solution)/shard_map/ppermute | solution.py:25
  87.1 3.3 %prior_grad.1 = f32[4,2048,128]{2,1,0:T(8,128)} custom-call(s32[32,20]{1,0:T(8,128)S(1)} %copy.17.table_ref, s32[1]{0:T(128)S(6)} %copy.25.window_ref, bf16[2048,128]{1,0:T(8,128)(2,1)S(1)} %far.3.mine_ref, bf16[2048,128]{1,0:T(8,128)(2,1)S(1)} %collective-permute-done.13.other_ref), custom_call_target="tpu_custom_call" | custom-call | flops 1048576 | bytes 4194304 | tf_op jit(solution)/shard_map/prior_grad/pallas_call | solution.py:466
  (55 shorter events, 12.7 us)
Async XLA Ops:
  0.6 1.0 %copy-start.10 = (bf16[128,8,128]{2,1,0:T(8,128)(2,1)S(1)}, bf16[128,8,128]{2,1,0:T(8,128)(2,1)}, u32[]{:S(2)}) copy-start(bf16[128,8,128]{2,1,0:T(8,128)(2,1)} %refs_0_.1) | copy-start | bytes 786436
  1.6 0.9 %copy-start.11 = (bf16[128,8,128]{2,1,0:T(8,128)(2,1)S(1)}, bf16[128,8,128]{2,1,0:T(8,128)(2,1)}, u32[]{:S(2)}) copy-start(bf16[128,8,128]{2,1,0:T(8,128)(2,1)} %refs_1_.1) | copy-start | bytes 786436
  2.9 5.7 %collective-permute-start.3 = (bf16[2,128,128]{2,1,0:T(8,128)(2,1)S(1)}, bf16[2,128,128]{2,1,0:T(8,128)(2,1)S(1)}, u32[]{:S(2)}, u32[]{:S(2)}) collective-permute-start(bf16[2,128,128]{2,1,0:T(8,128)(2,1)S(1)} %get-tuple-element.41), channel_id=1, source_target_pairs={{0,1},{1,0},{2,3},{3,2},{4,5},{5,4},{6,7},{7,6},{8,9},{9,8},{10,11... | collective-permute-start | bytes 196616 | tf_op jit(solution)/shard_map/ppermute | solution.py:25
  6.0 7.3 %collective-permute-start.4 = (bf16[2,128,128]{2,1,0:T(8,128)(2,1)S(1)}, bf16[2,128,128]{2,1,0:T(8,128)(2,1)S(1)}, u32[]{:S(2)}, u32[]{:S(2)}) collective-permute-start(bf16[2,128,128]{2,1,0:T(8,128)(2,1)S(1)} %get-tuple-element.42), channel_id=1, source_target_pairs={{0,2},{1,3},{2,0},{3,1},{4,6},{5,7},{6,4},{7,5},{8,10},{9,11},{10,... | collective-permute-start | bytes 196616 | tf_op jit(solution)/shard_map/ppermute | solution.py:25
  8.6 6.1 %collective-permute-start.5 = (bf16[2,128,128]{2,1,0:T(8,128)(2,1)S(1)}, bf16[2,128,128]{2,1,0:T(8,128)(2,1)S(1)}, u32[]{:S(2)}, u32[]{:S(2)}) collective-permute-start(bf16[2,128,128]{2,1,0:T(8,128)(2,1)S(1)} %get-tuple-element.43), channel_id=1, source_target_pairs={{0,3},{1,2},{2,1},{3,0},{4,7},{5,6},{6,5},{7,4},{8,11},{9,10},{10,... | collective-permute-start | bytes 196616 | tf_op jit(solution)/shard_map/ppermute | solution.py:25
  14.7 1.6 %copy-start = (bf16[512,2048]{1,0:T(8,128)(2,1)S(1)}, bf16[512,2048]{1,0:T(8,128)(2,1)}, u32[]{:S(2)}) copy-start(bf16[512,2048]{1,0:T(8,128)(2,1)} %x_ref.6) | copy-start | bytes 6291460
  16.2 9.1 %copy-start.2 = (bf16[512,2048]{1,0:T(8,128)(2,1)S(1)}, bf16[512,2048]{1,0:T(8,128)(2,1)}, u32[]{:S(2)}) copy-start(bf16[512,2048]{1,0:T(8,128)(2,1)} %x_ref.7) | copy-start | bytes 6291460
  16.8 9.2 %collective-permute-start.10 = (bf16[2048,128]{1,0:T(8,128)(2,1)S(1)}, bf16[2048,128]{1,0:T(8,128)(2,1)S(1)}, u32[]{:S(2)}, u32[]{:S(2)}) collective-permute-start(bf16[2048,128]{1,0:T(8,128)(2,1)S(1)} %get-tuple-element.53.a_ref), channel_id=1, source_target_pairs={{0,4},{4,0},{8,12},{12,8},{16,20},{20,16},{24,28},{28,24},{1,5},{5... | collective-permute-start | bytes 1572872 | tf_op jit(solution)/shard_map/ppermute | solution.py:25
  16.9 5.9 %collective-permute-start = (bf16[2,128,128]{2,1,0:T(8,128)(2,1)S(1)}, bf16[2,128,128]{2,1,0:T(8,128)(2,1)S(1)}, u32[]{:S(2)}, u32[]{:S(2)}) collective-permute-start(bf16[2,128,128]{2,1,0:T(8,128)(2,1)S(1)} %get-tuple-element.36), channel_id=1, source_target_pairs={{0,1},{1,0},{2,3},{3,2},{4,5},{5,4},{6,7},{7,6},{8,9},{9,8},{10,11... | collective-permute-start | bytes 196616 | tf_op jit(solution)/shard_map/ppermute | solution.py:25
  17.0 5.8 %collective-permute-start.1 = (bf16[2,128,128]{2,1,0:T(8,128)(2,1)S(1)}, bf16[2,128,128]{2,1,0:T(8,128)(2,1)S(1)}, u32[]{:S(2)}, u32[]{:S(2)}) collective-permute-start(bf16[2,128,128]{2,1,0:T(8,128)(2,1)S(1)} %get-tuple-element.37), channel_id=1, source_target_pairs={{0,2},{1,3},{2,0},{3,1},{4,6},{5,7},{6,4},{7,5},{8,10},{9,11},{10,... | collective-permute-start | bytes 196616 | tf_op jit(solution)/shard_map/ppermute | solution.py:25
  19.3 6.1 %collective-permute-start.2 = (bf16[2,128,128]{2,1,0:T(8,128)(2,1)S(1)}, bf16[2,128,128]{2,1,0:T(8,128)(2,1)S(1)}, u32[]{:S(2)}, u32[]{:S(2)}) collective-permute-start(bf16[2,128,128]{2,1,0:T(8,128)(2,1)S(1)} %get-tuple-element.38), channel_id=1, source_target_pairs={{0,3},{1,2},{2,1},{3,0},{4,7},{5,6},{6,5},{7,4},{8,11},{9,10},{10,... | collective-permute-start | bytes 196616 | tf_op jit(solution)/shard_map/ppermute | solution.py:25
  26.0 16.8 %copy-start.12 = (s32[32,20]{0,1:T(8,128)S(1)}, s32[32,20]{0,1:T(8,128)}, u32[]{:S(2)}) copy-start(s32[32,20]{0,1:T(8,128)} %param.10) | copy-start | bytes 7684
  26.0 2.0 %collective-permute-start.6 = (bf16[2048,128]{1,0:T(8,128)(2,1)S(1)}, bf16[2048,128]{1,0:T(8,128)(2,1)S(1)}, u32[]{:S(2)}, u32[]{:S(2)}) collective-permute-start(bf16[2048,128]{1,0:T(8,128)(2,1)S(1)} %get-tuple-element.48.a_ref), channel_id=1, source_target_pairs={{0,4},{4,0},{8,12},{12,8},{16,20},{20,16},{24,28},{28,24},{1,5},{5... | collective-permute-start | bytes 1572872 | tf_op jit(solution)/shard_map/ppermute | solution.py:25
  26.2 9.2 %collective-permute-start.11 = (bf16[1024,128]{1,0:T(8,128)(2,1)S(1)}, bf16[1024,128]{1,0:T(8,128)(2,1)S(1)}, u32[]{:S(2)}, u32[]{:S(2)}) collective-permute-start(bf16[1024,128]{1,0:T(8,128)(2,1)S(1)} %combine.6.a_ref), channel_id=1, source_target_pairs={{0,8},{4,12},{8,0},{12,4},{16,24},{20,28},{24,16},{28,20},{1,9},{5... | collective-permute-start | bytes 786440 | tf_op jit(solution)/shard_map/ppermute | solution.py:25
  28.8 21.9 %copy-start.1 = (bf16[512,2048]{1,0:T(8,128)(2,1)S(1)}, bf16[512,2048]{1,0:T(8,128)(2,1)}, u32[]{:S(2)}) copy-start(bf16[512,2048]{1,0:T(8,128)(2,1)} %x_ref.6) | copy-start | bytes 6291460
  28.8 11.7 %collective-permute-start.7 = (bf16[1024,128]{1,0:T(8,128)(2,1)S(1)}, bf16[1024,128]{1,0:T(8,128)(2,1)S(1)}, u32[]{:S(2)}, u32[]{:S(2)}) collective-permute-start(bf16[1024,128]{1,0:T(8,128)(2,1)S(1)} %combine.4.a_ref), channel_id=1, source_target_pairs={{0,8},{4,12},{8,0},{12,4},{16,24},{20,28},{24,16},{28,20},{1,9},{5... | collective-permute-start | bytes 786440 | tf_op jit(solution)/shard_map/ppermute | solution.py:25
  35.4 5.9 %copy-start.8 = (bf16[1024,128]{1,0:T(8,128)(2,1)}, bf16[1024,128]{1,0:T(8,128)(2,1)S(1)}, u32[]{:S(2)}) copy-start(bf16[1024,128]{1,0:T(8,128)(2,1)S(1)} %collective-permute-done.11.b_ref.refs_0_) | copy-start | bytes 786436
  36.2 7.6 %collective-permute-start.12 = (bf16[1024,128]{1,0:T(8,128)(2,1)}, bf16[1024,128]{1,0:T(8,128)(2,1)}, u32[]{:S(2)}, u32[]{:S(2)}) collective-permute-start(bf16[1024,128]{1,0:T(8,128)(2,1)} %combine.7.refs_2_), channel_id=1, source_target_pairs={{0,16},{4,20},{8,24},{12,28},{16,0},{20,4},{24,8},{28,12},{1,17},{... | collective-permute-start | bytes 786440 | tf_op jit(solution)/shard_map/ppermute | solution.py:25
  41.3 8.2 %collective-permute-start.8 = (bf16[1024,128]{1,0:T(8,128)(2,1)}, bf16[1024,128]{1,0:T(8,128)(2,1)}, u32[]{:S(2)}, u32[]{:S(2)}) collective-permute-start(bf16[1024,128]{1,0:T(8,128)(2,1)} %combine.5), channel_id=1, source_target_pairs={{0,16},{4,20},{8,24},{12,28},{16,0},{20,4},{24,8},{28,12},{1,17},{... | collective-permute-start | bytes 786440 | tf_op jit(solution)/shard_map/ppermute | solution.py:25
  43.8 1.0 %copy-start.9 = (bf16[1024,128]{1,0:T(8,128)(2,1)S(1)}, bf16[1024,128]{1,0:T(8,128)(2,1)}, u32[]{:S(2)}) copy-start(bf16[1024,128]{1,0:T(8,128)(2,1)} %copy-done.8) | copy-start | bytes 786436
  46.0 32.3 %collective-permute-start.13 = (bf16[2048,128]{1,0:T(8,128)(2,1)S(1)}, bf16[2048,128]{1,0:T(8,128)(2,1)S(1)}, u32[]{:S(2)}, u32[]{:S(2)}) collective-permute-start(bf16[2048,128]{1,0:T(8,128)(2,1)S(1)} %far.3.mine_ref), channel_id=1, source_target_pairs={{0,4},{4,0},{8,12},{12,8},{16,20},{20,16},{24,28},{28,24},{1,5},{5... | collective-permute-start | bytes 1572872 | tf_op jit(solution)/shard_map/ppermute | solution.py:25
  50.6 18.6 %collective-permute-start.9 = (bf16[1024,128]{1,0:T(8,128)(2,1)S(1)}, bf16[1024,128]{1,0:T(8,128)(2,1)S(1)}, u32[]{:S(2)}, u32[]{:S(2)}) collective-permute-start(bf16[1024,128]{1,0:T(8,128)(2,1)S(1)} %far.2.mine_ref), channel_id=1, source_target_pairs={{0,4},{4,0},{8,12},{12,8},{16,20},{20,16},{24,28},{28,24},{1,5},{5... | collective-permute-start | bytes 786440 | tf_op jit(solution)/shard_map/ppermute | solution.py:25
  50.7 1.6 %copy-start.3 = (bf16[512,2048]{1,0:T(8,128)(2,1)S(1)}, bf16[512,2048]{1,0:T(8,128)(2,1)}, u32[]{:S(2)}) copy-start(bf16[512,2048]{1,0:T(8,128)(2,1)} %x_ref.7) | copy-start | bytes 6291460
  63.6 4.3 %copy-start.5 = (bf16[4,32,64,128]{3,2,1,0:T(8,128)(2,1)S(1)}, bf16[4,32,64,128]{3,2,1,0:T(8,128)(2,1)}, u32[]{:S(2)}) copy-start(bf16[4,32,64,128]{3,2,1,0:T(8,128)(2,1)} %param.12) | copy-start | bytes 6291460
  63.6 4.3 %copy-start.7 = (bf16[2048,128]{1,0:T(8,128)(2,1)S(1)}, bf16[2048,128]{1,0:T(8,128)(2,1)}, u32[]{:S(2)}) copy-start(bf16[2048,128]{1,0:T(8,128)(2,1)} %copy-done.6) | copy-start | bytes 1572868
  69.2 9.1 %copy-start.4 = (bf16[512,2048]{1,0:T(8,128)(2,1)S(1)}, bf16[512,2048]{1,0:T(8,128)(2,1)}, u32[]{:S(2)}) copy-start(bf16[512,2048]{1,0:T(8,128)(2,1)} %x_ref.7) | copy-start | bytes 6291460
  72.8 12.2 %collective-permute-start.17 = (bf16[2,128,128]{2,1,0:T(8,128)(2,1)S(1)}, bf16[2,128,128]{2,1,0:T(8,128)(2,1)S(1)}, u32[]{:S(2)}, u32[]{:S(2)}) collective-permute-start(bf16[2,128,128]{2,1,0:T(8,128)(2,1)S(1)} %get-tuple-element.62), channel_id=1, source_target_pairs={{0,1},{1,0},{2,3},{3,2},{4,5},{5,4},{6,7},{7,6},{8,9},{9,8},{10,11... | collective-permute-start | bytes 196616 | tf_op jit(solution)/shard_map/ppermute | solution.py:25
  75.4 10.7 %collective-permute-start.18 = (bf16[2,128,128]{2,1,0:T(8,128)(2,1)S(1)}, bf16[2,128,128]{2,1,0:T(8,128)(2,1)S(1)}, u32[]{:S(2)}, u32[]{:S(2)}) collective-permute-start(bf16[2,128,128]{2,1,0:T(8,128)(2,1)S(1)} %get-tuple-element.63), channel_id=1, source_target_pairs={{0,2},{1,3},{2,0},{3,1},{4,6},{5,7},{6,4},{7,5},{8,10},{9,11},{10,... | collective-permute-start | bytes 196616 | tf_op jit(solution)/shard_map/ppermute | solution.py:25
  77.1 9.1 %collective-permute-start.19 = (bf16[2,128,128]{2,1,0:T(8,128)(2,1)S(1)}, bf16[2,128,128]{2,1,0:T(8,128)(2,1)S(1)}, u32[]{:S(2)}, u32[]{:S(2)}) collective-permute-start(bf16[2,128,128]{2,1,0:T(8,128)(2,1)S(1)} %get-tuple-element.64), channel_id=1, source_target_pairs={{0,3},{1,2},{2,1},{3,0},{4,7},{5,6},{6,5},{7,4},{8,11},{9,10},{10,... | collective-permute-start | bytes 196616 | tf_op jit(solution)/shard_map/ppermute | solution.py:25
  81.7 8.7 %collective-permute-start.14 = (bf16[2,128,128]{2,1,0:T(8,128)(2,1)S(1)}, bf16[2,128,128]{2,1,0:T(8,128)(2,1)S(1)}, u32[]{:S(2)}, u32[]{:S(2)}) collective-permute-start(bf16[2,128,128]{2,1,0:T(8,128)(2,1)S(1)} %get-tuple-element.58), channel_id=1, source_target_pairs={{0,1},{1,0},{2,3},{3,2},{4,5},{5,4},{6,7},{7,6},{8,9},{9,8},{10,11... | collective-permute-start | bytes 196616 | tf_op jit(solution)/shard_map/ppermute | solution.py:25
  82.4 8.0 %collective-permute-start.15 = (bf16[2,128,128]{2,1,0:T(8,128)(2,1)S(1)}, bf16[2,128,128]{2,1,0:T(8,128)(2,1)S(1)}, u32[]{:S(2)}, u32[]{:S(2)}) collective-permute-start(bf16[2,128,128]{2,1,0:T(8,128)(2,1)S(1)} %get-tuple-element.59), channel_id=1, source_target_pairs={{0,2},{1,3},{2,0},{3,1},{4,6},{5,7},{6,4},{7,5},{8,10},{9,11},{10,... | collective-permute-start | bytes 196616 | tf_op jit(solution)/shard_map/ppermute | solution.py:25
  84.9 6.2 %collective-permute-start.16 = (bf16[2,128,128]{2,1,0:T(8,128)(2,1)S(1)}, bf16[2,128,128]{2,1,0:T(8,128)(2,1)S(1)}, u32[]{:S(2)}, u32[]{:S(2)}) collective-permute-start(bf16[2,128,128]{2,1,0:T(8,128)(2,1)S(1)} %get-tuple-element.60), channel_id=1, source_target_pairs={{0,3},{1,2},{2,1},{3,0},{4,7},{5,6},{6,5},{7,4},{8,11},{9,10},{10,... | collective-permute-start | bytes 196616 | tf_op jit(solution)/shard_map/ppermute | solution.py:25
  (1 other events, 0.8 us)
where the time goes:
time: 92.4 us; the launch traced here: 92.1 us
  Pallas kernels  34.8 us (38%)
  starting transfers between devices  25.5 us (28%)
  waiting for transfers between devices  23.4 us (25%)
  local copies, waits for them, and re-layouts  6.93 us (7%)
  between operations  1.53 us (2%)
    ppermute x20, starting transfers between devices, swap_with(): lax.ppermute(array, axis, [(i, i ^ mask) for i in range(lax.axis_size(axi...  25.5 us
    ppermute x20, waiting for transfers between devices, swap_with(): lax.ppermute(array, axis, [(i, i ^ mask) for i in range(lax.axis_size(axi...  23.4 us
    pallas_call x2, Pallas kernels, intra(): pl.pallas_call(functools.partial(intra_kernel, base=base, head_dim=head_d...  8.49 us
    pallas_call x2, Pallas kernels, finish(): pl.pallas_call(functools.partial(finish_kernel, pieces=pieces, halves=wid...  7.02 us
    unnamed x27, local copies, waits for them, and re-layouts  6.93 us
    pallas_call x2, Pallas kernels, gram(): pl.pallas_call(functools.partial(gram_kernel, base=base, head_dim=head_di...  6.37 us
    pallas_call x1, Pallas kernels, prior_grad(): pl.pallas_call(functools.partial(prior_kernel, head_dim=head_dim, level=l...  3.28 us
    pallas_call x2, Pallas kernels, far(): pl.pallas_call(functools.partial(far_kernel, level=level, gate=gate, head...  2.29 us
  transfers between devices with their start and end apart: 20, of which 10 were waited for; matrix products, arithmetic and copies ran while one was open for 0% of the time, Pallas kernels for 36%

commit v1 on v0

--- a/solution.py
+++ b/solution.py
@@ -14,6 +14,7 @@
 F32 = jnp.float32
 SMEM = pl.BlockSpec(memory_space=pltpu.SMEM)
 VMEM = pl.BlockSpec(memory_space=pltpu.VMEM)
+HBM = pl.BlockSpec(memory_space=pltpu.HBM)
 PARAMS = pltpu.CompilerParams(vmem_limit_bytes=24 << 20)
 
 
@@ -21,6 +22,10 @@
     return pltpu.with_memory_space_constraint(array, pltpu.VMEM)
 
 
+def far_off(array):
+    return pltpu.with_memory_space_constraint(array, pltpu.HBM)
+
+
 def swap_with(array, axis, mask):
     return lax.ppermute(array, axis, [(i, i ^ mask) for i in range(lax.axis_size(axis))])
 
@@ -46,7 +51,7 @@
 
 
 def weight(table_ref, head, level):
-    return table_ref[head, level].astype(F32) * 2.0 ** (-max(level - 1, 0) / 2)
+    return table_ref[level, head].astype(F32) * 2.0 ** (-max(level - 1, 0) / 2)
 
 
 def log2(number):
@@ -54,28 +59,45 @@
 
 
 def prep_kernel(*refs, pieces):
-    x_refs, outs, scratch = refs[:2], refs[2:-1], refs[-1]
+    x_refs, big, refs = refs[:2], refs[2:4], refs[4:]
+    outs, big_outs = refs[: 2 * pieces], refs[2 * pieces : 2 * pieces + 2]
+    raw, scratch, sems = refs[2 * pieces + 2 :]
     here = lax.axis_index("head")
-    for n, x_ref in enumerate(x_refs):
-        scratch[...] = jnp.swapaxes(x_ref[...].astype(F32), 0, 1)
+    copies = [pltpu.make_async_copy(x, raw.at[n], sems.at[n]) for n, x in enumerate(x_refs)]
+    copies += [
+        pltpu.make_async_copy(x, out, sems.at[2 + n])
+        for n, (x, out) in enumerate(zip(big, big_outs))
+    ]
+    for copy in copies:
+        copy.start()
+    for n in range(2):
+        copies[n].wait()
+        scratch[...] = jnp.swapaxes(raw[n].astype(F32), 0, 1)
         for r, out in enumerate(outs[n * pieces : (n + 1) * pieces]):
             take = out.shape[0]
             out[...] = scratch[pl.ds((here ^ r) * take, take)].astype(out.dtype)
-
-
-def prep(keys, queries, pieces):
+    copies[2].wait()
+    copies[3].wait()
+
+
+def prep(keys, queries, values, cotangent, pieces):
     rows, groups, state = keys.shape
     out = pl.pallas_call(
         functools.partial(prep_kernel, pieces=pieces),
-        in_specs=[VMEM] * 2,
-        out_specs=[VMEM] * (2 * pieces),
-        out_shape=[pltpu.VMEM((groups // pieces, rows, state), BF)] * (2 * pieces),
-        scratch_shapes=[pltpu.VMEM((groups, rows, state), F32)],
+        in_specs=[HBM] * 4,
+        out_specs=[VMEM] * (2 * pieces + 2),
+        out_shape=[pltpu.VMEM((groups // pieces, rows, state), BF)] * (2 * pieces)
+        + [pltpu.VMEM(values.shape, BF)] * 2,
+        scratch_shapes=[
+            pltpu.VMEM((2,) + keys.shape, BF),
+            pltpu.VMEM((groups, rows, state), F32),
+            pltpu.SemaphoreType.DMA((4,)),
+        ],
         compiler_params=PARAMS,
         cost_estimate=cost(10**6, 8 * keys.size),
         name="prep",
-    )(keys, queries)
-    return out[:pieces], out[pieces:]
+    )(*[far_off(x) for x in (keys, queries, values, cotangent)])
+    return out[:pieces], out[pieces : 2 * pieces], out[-2], out[-1]
 
 
 def states_kernel(x_ref, *refs):
@@ -369,55 +391,126 @@
     )(table, *[near_core(x) for x in partners + extra])
 
 
-def finish_kernel(
-    part_ref, r_ref, near_ref, mine_ref, other_ref, x_ref, *refs, pieces, halves, cols
-):
-    groups = r_ref.shape[0]
-    g_refs, o_ref, outs, acc = refs[:groups], refs[groups], refs[groups + 1 : -1], refs[-1]
-    group, step = pl.program_id(0), pl.program_id(1)
-    at = group * pl.num_programs(1) + step
-    is_mine = at // halves == lax.axis_index("seq") & 1
-    span = pl.ds(pl.multiple_of(at * cols, cols), cols)
-    half = pl.ds(pl.multiple_of(at % halves * cols, cols), cols)
-    flow = near_ref[span, :] + jnp.where(is_mine, mine_ref[half, :], other_ref[half, :]).astype(F32)
-    flow = flow.astype(BF)
-    o_ref[...] = (part_ref[:, span].astype(F32) + dot_nt(r_ref[group], flow)).astype(o_ref.dtype)
+def slope_kernel(near_ref, mine_ref, other_ref, x_ref, *refs, pieces):
+    groups = len(refs) - pieces - 2
+    g_refs, flow_ref, outs, acc = refs[:groups], refs[groups], refs[groups + 1 : -1], refs[-1]
+    half = mine_ref.shape[0]
+    half = flow_ref.shape[0] // 2
+    core = lax.axis_index("seq") & 1
+    for ref, at in ((mine_ref, core), (other_ref, 1 - core)):
+        rows = pl.ds(pl.multiple_of(at * half, half), half)
+        flow_ref[rows, :] = (near_ref[rows, :] + ref[pl.ds(0, half), :].astype(F32)).astype(BF)
+    width = x_ref.shape[1] // groups
     for g in range(groups):
-
-        @pl.when((step == 0) & (group == g))
-        def _():
-            acc[...] = g_refs[g][...]
-
-    acc[...] += dot_nn(x_ref[:, span], flow)
-
-    @pl.when(step == pl.num_programs(1) - 1)
-    def _():
+        span = slice(g * width, (g + 1) * width)
+        grad = g_refs[g][...] + dot_nn(x_ref[:, span], flow_ref[span, :])
         if pieces == 1:
-            outs[0][group] = acc[...].astype(BF)
+            outs[0][g] = grad.astype(BF)
         else:
+            acc[...] = grad
             here = lax.axis_index("head")
             size = outs[0].shape[1]
             for r, out in enumerate(outs):
                 rows = pl.ds(pl.multiple_of((here ^ r) * size, size), size)
-                out[group] = acc[rows, :].astype(BF)
-
-
-def finish(part, rows, near_flow, mine, other, x, grads, cols, pieces):
-    tok, width = part.shape
-    groups, _, state = rows.shape
-    steps = width // groups // cols
+                out[g] = acc[rows, :].astype(BF)
+
+
+def slope(near_flow, mine, other, x, grads, pieces):
+    tok, width = x.shape
+    groups = len(grads)
+    state = near_flow.shape[1]
     piece = (groups, tok // pieces, state)
-    return pl.pallas_call(
-        functools.partial(finish_kernel, pieces=pieces, halves=width // cols // 2, cols=cols),
-        grid=(groups, steps),
-        in_specs=[VMEM] * (6 + groups),
-        out_specs=[pl.BlockSpec((tok, cols), lambda g, j: (0, g * steps + j))] + [VMEM] * pieces,
-        out_shape=[shaped((tok, width), BF)] + [pltpu.VMEM(piece, BF)] * pieces,
+    flow, *parts = pl.pallas_call(
+        functools.partial(slope_kernel, pieces=pieces),
+        in_specs=[VMEM] * (4 + groups),
+        out_specs=[VMEM] * (1 + pieces),
+        out_shape=[pltpu.VMEM((width, state), BF)] + [pltpu.VMEM(piece, BF)] * pieces,
         scratch_shapes=[pltpu.VMEM((tok, state), F32)],
         compiler_params=PARAMS,
+        cost_estimate=cost(2 * tok * width * state, 2 * tok * width),
+        name="slope",
+    )(near_flow, near_core(mine), near_core(other), x, *grads)
+    return flow, parts
+
+
+def outs_kernel(
+    table_ref, window_ref, mix_ref, q_ref, in_ref, dv_ref, k_ref, out_ref, mine_ref, other_ref,
+    *refs, cols, count, head_dim, level,
+):
+    parts, refs = refs[:-9], refs[-9:]
+    mix_hbm, dv_hbm, prior_hbm, grad_hbm, mix_sc, dv_sc, prior_sc, grad_sc, sems = refs
+    _, width = mix_ref.shape
+    groups = q_ref.shape[0]
+    chunks = width // cols
+    half = width // 2
+    core = lax.axis_index("seq") & 1
+    copies = []
+
+    def send(source, target):
+        copy = pltpu.make_async_copy(source, target, sems.at[len(copies)])
+        copy.start()
+        copies.append(copy)
+
+    for at in range(chunks):
+        rows = pl.ds(at * cols, cols)
+        first = half + at * cols % half
+        source = pl.ds(first, cols)
+        is_mine = core == at * cols // half
+        total = jnp.where(is_mine, mine_ref[source, :], other_ref[source, :]).astype(F32)
+        for h in range(cols // head_dim):
+            head = at * cols // head_dim + h
+            piece = total[h * head_dim : (h + 1) * head_dim]
+            for k in range(count):
+                bit = (window_ref[0] >> k & 1).astype(F32)
+                prior_sc[k, pl.ds(head * head_dim, head_dim), :] = piece * (
+                    weight(table_ref, head, level + k) * bit
+                )
+        send(prior_sc.at[:, rows, :], prior_hbm.at[:, rows, :])
+    for part, r, flow, sc, hbm in (
+        (mix_ref, q_ref, in_ref, mix_sc, mix_hbm), (dv_ref, k_ref, out_ref, dv_sc, dv_hbm)
+    ):
+        for at in range(chunks):
+            span = pl.ds(at * cols, cols)
+            added = dot_nt(r[at * cols * groups // width], flow[span, :])
+            sc[:, span] = (part[:, span].astype(F32) + added).astype(BF)
+            send(sc.at[:, span], hbm.at[:, span])
+    if parts:
+        here = lax.axis_index("head")
+        take = parts[0].shape[0]
+        rows = parts[0].shape[1]
+        stacked = grad_sc.at[0]
+        for r, part in enumerate(parts):
+            stacked[pl.ds((here ^ r) * take, take)] = part[...].astype(F32)
+        final = grad_sc.at[1].reshape(rows, take * len(parts), parts[0].shape[2])
+        final[...] = jnp.swapaxes(stacked[...], 0, 1)
+        send(final, grad_hbm)
+    for copy in copies:
+        copy.wait()
+
+
+def outs(table, window, mix, queries, inflow, dv, keys, outflow, mine, other, parts, count, level, head_dim, cols):
+    tok, width = mix.shape
+    state = inflow.shape[1]
+    chunks = width // cols
+    groups, rows = (parts[0].shape[0] * len(parts), parts[0].shape[1]) if parts else (8, 8)
+    return pl.pallas_call(
+        functools.partial(outs_kernel, cols=cols, count=count, head_dim=head_dim, level=level),
+        in_specs=[SMEM, SMEM] + [VMEM] * (8 + len(parts)),
+        out_specs=[HBM] * 4,
+        out_shape=[
+            pltpu.HBM((tok, width), BF), pltpu.HBM((tok, width), BF),
+            pltpu.HBM((count, width, state), F32), pltpu.HBM((rows, groups, state), F32),
+        ],
+        scratch_shapes=[
+            pltpu.VMEM((tok, width), BF), pltpu.VMEM((tok, width), BF),
+            pltpu.VMEM((count, width, state), F32), pltpu.VMEM((2, groups, rows, state), F32),
+            pltpu.SemaphoreType.DMA((3 * chunks + 1,)),
+        ],
+        compiler_params=PARAMS,
         cost_estimate=cost(4 * tok * width * state, 6 * tok * width),
-        name="finish",
-    )(part, rows, near_flow, near_core(mine), near_core(other), x, *grads)
+        name="outs",
+    )(table, window, mix, queries, inflow, dv, keys, outflow, mine, other,
+      *[near_core(part) for part in parts])
 
 
 def gather_kernel(*refs):
@@ -444,37 +537,6 @@
     )(*[near_core(part) for part in parts])
 
 
-def prior_kernel(table_ref, window_ref, mine_ref, other_ref, o_ref, *, head_dim, level, halves):
-    at = pl.program_id(0)
-    size = o_ref.shape[1]
-    heads = size // head_dim
-    is_mine = at // halves == lax.axis_index("seq") & 1
-    rows = pl.ds(pl.multiple_of((halves + at % halves) * size, size), size)
-    total = jnp.where(is_mine, mine_ref[rows, :], other_ref[rows, :]).astype(F32)
-    for h in range(heads):
-        rows = slice(h * head_dim, (h + 1) * head_dim)
-        for k in range(o_ref.shape[0]):
-            bit = (window_ref[0] >> k & 1).astype(F32)
-            o_ref[k, rows, :] = total[rows] * (weight(table_ref, at * heads + h, level + k) * bit)
-
-
-def prior_grad(table, window, mine, other, count, level, head_dim, steps):
-    half = mine.shape[0] // 2
-    state = mine.shape[1]
-    halves = steps // 2
-    rows = half // halves
-    return pl.pallas_call(
-        functools.partial(prior_kernel, head_dim=head_dim, level=level, halves=halves),
-        grid=(steps,),
-        in_specs=[SMEM, SMEM, VMEM, VMEM],
-        out_specs=pl.BlockSpec((count, rows, state), lambda i: (0, i, 0)),
-        out_shape=shaped((count, 2 * half, state), F32),
-        compiler_params=PARAMS,
-        cost_estimate=cost(2 * count * half * state, 8 * count * half * state),
-        name="prior_grad",
-    )(table, window, near_core(mine), near_core(other))
-
-
 def mixer(
     values, group_keys, group_queries, level_table, window_index, prior_states, cotangent
 ):
@@ -482,6 +544,7 @@
     head_count = lax.axis_size("head")
     tok_rows = values.shape[0]
     heads_here = level_table.shape[0]
+    level_table = level_table.T
     head_dim = values.shape[1] // heads_here
     state_dim = group_keys.shape[2]
     group_count = group_keys.shape[1]
@@ -513,11 +576,13 @@
 
     if pieces == 1:
         key_parts, query_parts = rows_of(group_keys), rows_of(group_queries)
+        values, cotangent = near_core(values), near_core(cotangent)
     else:
-        key_parts, query_parts = prep(group_keys, group_queries, pieces)
+        key_parts, query_parts, values, cotangent = prep(
+            group_keys, group_queries, values, cotangent, pieces
+        )
         key_parts = scattered(*key_parts)
         query_parts = scattered(*query_parts)
-    values, cotangent = near_core(values), near_core(cotangent)
     grams = []
     for g in range(local_groups):
         grams.append(
@@ -556,27 +621,26 @@
         key_grads.append(key_grad)
     mix_part, dv_part = parts
 
-    def back(parts):
-        if pieces == 1:
-            part = parts[0].reshape(local_groups, head_count, -1, state_dim).swapaxes(0, 1)
-            part = lax.all_to_all(part, "head", split_axis=0, concat_axis=0).astype(F32)
-            part = part.reshape(group_count, repeats, -1, state_dim).sum(axis=1)
-            return part.swapaxes(0, 1)
-        parts = scattered(*parts)
-        return gather(parts)
-
-    mixer_out, *query_parts = finish(
-        mix_part, query_rows, in_near, in_mine, in_other, cotangent, query_grads, cols, pieces
+    def back(part):
+        part = part.reshape(local_groups, head_count, -1, state_dim).swapaxes(0, 1)
+        part = lax.all_to_all(part, "head", split_axis=0, concat_axis=0).astype(F32)
+        part = part.reshape(group_count, repeats, -1, state_dim).sum(axis=1)
+        return part.swapaxes(0, 1)
+
+    inflow, query_parts = slope(in_near, in_mine, in_other, cotangent, query_grads, pieces)
+    outflow, key_parts = slope(out_near, out_mine, out_other, values, key_grads, pieces)
+    if pieces > 1:
+        query_parts = scattered(*query_parts)
+        key_parts = scattered(*key_parts)
+    mixer_out, grad_values, grad_prior, grad_queries = outs(
+        level_table, window_index, mix_part, query_rows, inflow, dv_part, key_rows, outflow,
+        out_mine, out_other, query_parts if pieces > 1 else [], prior_count, 1 + log_window,
+        head_dim, cols,
     )
-    grad_queries = back(query_parts)
-    grad_values, *key_parts = finish(
-        dv_part, key_rows, out_near, out_mine, out_other, values, key_grads, cols, pieces
-    )
-    grad_keys = back(key_parts)
-    grad_prior = prior_grad(
-        level_table, window_index, out_mine, out_other, prior_count, 1 + log_window, head_dim,
-        width // cols,
-    )
+    if pieces > 1:
+        grad_keys = gather(key_parts)
+    else:
+        grad_queries, grad_keys = back(query_parts[0]), back(key_parts[0])
     return (mixer_out, grad_values, grad_keys, grad_queries, grad_prior.reshape(prior_states.shape))
 
 

time: 92.4 us -> 82.5 us (0.89)
  local copies, waits for them, and re-layouts: 6.93 us -> 0.01 us
  Pallas kernels: 34.8 us -> 29.7 us
  waiting for transfers between devices: 23.4 us -> 25.4 us
    unnamed x27 -> x4, local copies, waits for them, and re-layouts: 6.93 us -> 0.01 us
    ppermute x20, waiting for transfers between devices: 23.4 us -> 25.4 us  [swap_with(): lax.ppermute(array, axis, [(i, i ^ mask) for i in range(lax.axis_size(axi...]
    pallas_call x4, Pallas kernels: 10.6 us -> 8.83 us  [the longest x1 4.65 us: outs(): pl.pallas_call(functools.partial(outs_kernel, cols=cols, count=count, hea...]
    pallas_call x4, Pallas kernels: 1.69 us -> 0.27 us  [combine(): pl.pallas_call(combine_kernel, in_specs=[VMEM] * 2, out_specs=VMEM, out_s...]
    pallas_call x2 -> x1, Pallas kernels: 1.95 us -> 0.97 us  [gather(): pl.pallas_call(gather_kernel, in_specs=[VMEM] * len(parts), out_specs=pl....]
  transfers between devices with their start and end apart: 20 -> 20, of which waited for: 10 -> 10; matrix products, arithmetic and copies ran while one was open for 0% -> 0% of each run, Pallas kernels for 36% -> 31%
where the time goes in v1:
time: 82.5 us; the launch traced here: 82.4 us
  Pallas kernels  29.7 us (36%)
  starting transfers between devices  25.7 us (31%)
  waiting for transfers between devices  25.4 us (31%)
  between operations  1.51 us (2%)
    ppermute x20, starting transfers between devices, swap_with(): lax.ppermute(array, axis, [(i, i ^ mask) for i in range(lax.axis_size(axi...  25.7 us
    ppermute x20, waiting for transfers between devices, swap_with(): lax.ppermute(array, axis, [(i, i ^ mask) for i in range(lax.axis_size(axi...  25.4 us
    pallas_call x2, Pallas kernels, intra(): pl.pallas_call(functools.partial(intra_kernel, base=base, head_dim=head_d...  8.49 us
    pallas_call x2, Pallas kernels, gram(): pl.pallas_call(functools.partial(gram_kernel, base=base, head_dim=head_di...  6.18 us
    pallas_call x1, Pallas kernels, outs(): pl.pallas_call(functools.partial(outs_kernel, cols=cols, count=count, hea...  4.65 us
    pallas_call x1, Pallas kernels, prep(): pl.pallas_call(functools.partial(prep_kernel, pieces=pieces), in_specs=[H...  2.44 us
    pallas_call x2, Pallas kernels, near(): pl.pallas_call(functools.partial(near_kernel, level=level, gate=gate, hea...  2.06 us
    pallas_call x2, Pallas kernels, far(): pl.pallas_call(functools.partial(far_kernel, level=level, gate=gate, head...  1.77 us
  transfers between devices with their start and end apart: 20, of which 10 were waited for; matrix products, arithmetic and copies ran while one was open for 0% of the time, Pallas kernels for 31%

profile of v1, /device:TPU:0, one launch (start us, length us, event | category | flops | bytes accessed | tf_op | source)
XLA Modules:
  0.0 82.4 jit_solution(4708940872611678919)
XLA Ops:
  0.6 2.4 %prep.1 = (bf16[2,128,128]{2,1,0:T(8,128)(2,1)S(1)}, bf16[2,128,128]{2,1,0:T(8,128)(2,1)S(1)}, bf16[2,128,128]{2,1,0:T(8,128)(2,1)S(1)}, bf16[2,128,128]{2,1,0:T...) custom-call(bf16[128,8,128]{2,1,0:T(8,128)(2,1)} %refs_0_.1, ...), custom_call_target="tpu_custom_call" | custom-call | flops 1000000 | bytes 1048576 | tf_op jit(solution)/shard_map/prep/pallas_call | solution.py:85
  3.1 3.1 %collective-permute-start.3 = (bf16[2,128,128]{2,1,0:T(8,128)(2,1)S(1)}, bf16[2,128,128]{2,1,0:T(8,128)(2,1)S(1)}, u32[]{:S(2)}, u32[]{:S(2)}) collective-permute-start(bf16[2,128,128]{2,1,0:T(8,128)(2,1)S(1)} %get-tuple-element.49), channel_id=1, source_target_pairs={{0,1},{1,0},{2,3},{3,2},{4,5},{5,4},{6,7},{7,6},{8,9},{9,8},{10,11... | collective-permute-start | bytes 196616 | tf_op jit(solution)/shard_map/ppermute | solution.py:30
  6.2 2.6 %collective-permute-start.4 = (bf16[2,128,128]{2,1,0:T(8,128)(2,1)S(1)}, bf16[2,128,128]{2,1,0:T(8,128)(2,1)S(1)}, u32[]{:S(2)}, u32[]{:S(2)}) collective-permute-start(bf16[2,128,128]{2,1,0:T(8,128)(2,1)S(1)} %get-tuple-element.50), channel_id=1, source_target_pairs={{0,2},{1,3},{2,0},{3,1},{4,6},{5,7},{6,4},{7,5},{8,10},{9,11},{10,... | collective-permute-start | bytes 196616 | tf_op jit(solution)/shard_map/ppermute | solution.py:30
  8.8 4.7 %collective-permute-done.4.refs_2_ = bf16[2,128,128]{2,1,0:T(8,128)(2,1)S(1)} collective-permute-done((bf16[2,128,128]{2,1,0:T(8,128)(2,1)S(1)}, bf16[2,128,128]{2,1,0:T(8,128)(2,1)S(1)}, u32[]{:S(2)}, u32[]{:S(2)}) %collective-permute-start.4) | collective-permute-done | bytes 65568 | tf_op jit(solution)/shard_map/ppermute | solution.py:30
  13.5 1.4 %collective-permute-done.5.refs_3_ = bf16[2,128,128]{2,1,0:T(8,128)(2,1)S(1)} collective-permute-done((bf16[2,128,128]{2,1,0:T(8,128)(2,1)S(1)}, bf16[2,128,128]{2,1,0:T(8,128)(2,1)S(1)}, u32[]{:S(2)}, u32[]{:S(2)}) %collective-permute-start.5) | collective-permute-done | bytes 65568 | tf_op jit(solution)/shard_map/ppermute | solution.py:30
  15.6 2.3 %collective-permute-start.1 = (bf16[2,128,128]{2,1,0:T(8,128)(2,1)S(1)}, bf16[2,128,128]{2,1,0:T(8,128)(2,1)S(1)}, u32[]{:S(2)}, u32[]{:S(2)}) collective-permute-start(bf16[2,128,128]{2,1,0:T(8,128)(2,1)S(1)} %get-tuple-element.45), channel_id=1, source_target_pairs={{0,2},{1,3},{2,0},{3,1},{4,6},{5,7},{6,4},{7,5},{8,10},{9,11},{10,... | collective-permute-start | bytes 196616 | tf_op jit(solution)/shard_map/ppermute | solution.py:30
  17.9 2.0 %collective-permute-start.2 = (bf16[2,128,128]{2,1,0:T(8,128)(2,1)S(1)}, bf16[2,128,128]{2,1,0:T(8,128)(2,1)S(1)}, u32[]{:S(2)}, u32[]{:S(2)}) collective-permute-start(bf16[2,128,128]{2,1,0:T(8,128)(2,1)S(1)} %get-tuple-element.46), channel_id=1, source_target_pairs={{0,3},{1,2},{2,1},{3,0},{4,7},{5,6},{6,5},{7,4},{8,11},{9,10},{10,... | collective-permute-start | bytes 196616 | tf_op jit(solution)/shard_map/ppermute | solution.py:30
  20.0 1.4 %collective-permute-done.refs_1_ = bf16[2,128,128]{2,1,0:T(8,128)(2,1)S(1)} collective-permute-done((bf16[2,128,128]{2,1,0:T(8,128)(2,1)S(1)}, bf16[2,128,128]{2,1,0:T(8,128)(2,1)S(1)}, u32[]{:S(2)}, u32[]{:S(2)}) %collective-permute-start) | collective-permute-done | bytes 65568 | tf_op jit(solution)/shard_map/ppermute | solution.py:30
  21.4 2.6 %collective-permute-done.2.refs_3_ = bf16[2,128,128]{2,1,0:T(8,128)(2,1)S(1)} collective-permute-done((bf16[2,128,128]{2,1,0:T(8,128)(2,1)S(1)}, bf16[2,128,128]{2,1,0:T(8,128)(2,1)S(1)}, u32[]{:S(2)}, u32[]{:S(2)}) %collective-permute-start.2) | collective-permute-done | bytes 65568 | tf_op jit(solution)/shard_map/ppermute | solution.py:30
  24.8 1.6 %collective-permute-start.11 = (bf16[1024,128]{1,0:T(8,128)(2,1)S(1)}, bf16[1024,128]{1,0:T(8,128)(2,1)S(1)}, u32[]{:S(2)}, u32[]{:S(2)}) collective-permute-start(bf16[1024,128]{1,0:T(8,128)(2,1)S(1)} %combine.6.a_ref), channel_id=1, source_target_pairs={{0,8},{4,12},{8,0},{12,4},{16,24},{20,28},{24,16},{28,20},{1,9},{5... | collective-permute-start | bytes 786440 | tf_op jit(solution)/shard_map/ppermute | solution.py:30
  26.6 1.6 %collective-permute-start.7 = (bf16[1024,128]{1,0:T(8,128)(2,1)S(1)}, bf16[1024,128]{1,0:T(8,128)(2,1)S(1)}, u32[]{:S(2)}, u32[]{:S(2)}) collective-permute-start(bf16[1024,128]{1,0:T(8,128)(2,1)S(1)} %combine.4.a_ref), channel_id=1, source_target_pairs={{0,8},{4,12},{8,0},{12,4},{16,24},{20,28},{24,16},{28,20},{1,9},{5... | collective-permute-start | bytes 786440 | tf_op jit(solution)/shard_map/ppermute | solution.py:30
  28.2 5.8 %collective-permute-done.11.b_ref.refs_0_ = bf16[1024,128]{1,0:T(8,128)(2,1)S(1)} collective-permute-done((bf16[1024,128]{1,0:T(8,128)(2,1)S(1)}, bf16[1024,128]{1,0:T(8,128)(2,1)S(1)}, u32[]{:S(2)}, u32[]{:S(2)}) %collective-permute-start.11) | collective-permute-done | bytes 262176 | tf_op jit(solution)/shard_map/ppermute | solution.py:30
  34.1 1.6 %collective-permute-start.12 = (bf16[1024,128]{1,0:T(8,128)(2,1)S(1)}, bf16[1024,128]{1,0:T(8,128)(2,1)S(1)}, u32[]{:S(2)}, u32[]{:S(2)}) collective-permute-start(bf16[1024,128]{1,0:T(8,128)(2,1)S(1)} %combine.7.refs_2_), channel_id=1, source_target_pairs={{0,16},{4,20},{8,24},{12,28},{16,0},{20,4},{24,8},{28,12},{1,17},{... | collective-permute-start | bytes 786440 | tf_op jit(solution)/shard_map/ppermute | solution.py:30
  35.7 3.5 %collective-permute-done.7.b_ref.refs_0_ = bf16[1024,128]{1,0:T(8,128)(2,1)S(1)} collective-permute-done((bf16[1024,128]{1,0:T(8,128)(2,1)S(1)}, bf16[1024,128]{1,0:T(8,128)(2,1)S(1)}, u32[]{:S(2)}, u32[]{:S(2)}) %collective-permute-start.7) | collective-permute-done | bytes 262176 | tf_op jit(solution)/shard_map/ppermute | solution.py:30
  39.2 1.6 %collective-permute-start.8 = (bf16[1024,128]{1,0:T(8,128)(2,1)S(1)}, bf16[1024,128]{1,0:T(8,128)(2,1)S(1)}, u32[]{:S(2)}, u32[]{:S(2)}) collective-permute-start(bf16[1024,128]{1,0:T(8,128)(2,1)S(1)} %combine.5), channel_id=1, source_target_pairs={{0,16},{4,20},{8,24},{12,28},{16,0},{20,4},{24,8},{28,12},{1,17},{... | collective-permute-start | bytes 786440 | tf_op jit(solution)/shard_map/ppermute | solution.py:30
  41.5 0.9 %far.3.mine_ref = bf16[2048,128]{1,0:T(8,128)(2,1)S(1)} custom-call(s32[20,32]{1,0:T(8,128)S(1)} %bitcast.4, bf16[1024,128]{1,0:T(8,128)(2,1)S(1)} %collective-permute-done.11.b_ref.refs_0_, bf16[1024,128]{1,0:T(8,128)(2,1)S(1)} %collective-permute-done.12.refs_1_, bf16[1024,128]{1,0:T(8,128)(2,1)S(1)} %combine.7.refs_2_), custom_call_target="tpu_custom_call" | custom-call | flops 1310720 | bytes 1048576 | tf_op jit(solution)/shard_map/far/pallas_call | solution.py:381
  42.5 4.6 %collective-permute-done.8.refs_1_ = bf16[1024,128]{1,0:T(8,128)(2,1)S(1)} collective-permute-done((bf16[1024,128]{1,0:T(8,128)(2,1)S(1)}, bf16[1024,128]{1,0:T(8,128)(2,1)S(1)}, u32[]{:S(2)}, u32[]{:S(2)}) %collective-permute-start.8) | collective-permute-done | bytes 262176 | tf_op jit(solution)/shard_map/ppermute | solution.py:30
  47.1 0.9 %far.2.mine_ref = bf16[1024,128]{1,0:T(8,128)(2,1)S(1)} custom-call(s32[20,32]{1,0:T(8,128)S(1)} %bitcast.5, bf16[1024,128]{1,0:T(8,128)(2,1)S(1)} %collective-permute-done.7.b_ref.refs_0_, bf16[1024,128]{1,0:T(8,128)(2,1)S(1)} %collective-permute-done.8.refs_1_), custom_call_target="tpu_custom_call" | custom-call | flops 1310720 | bytes 1048576 | tf_op jit(solution)/shard_map/far/pallas_call | solution.py:381
  48.0 3.1 %gram.2.g_ref = bf16[512,512]{1,0:T(8,128)(2,1)S(1)} custom-call(s32[20,32]{1,0:T(8,128)S(1)} %bitcast.6, bf16[512,2048]{1,0:T(8,128)(2,1)S(1)} %get-tuple-element.41.x_ref.v_ref, bf16[512,2048]{1,0:T(8,128)(2,1)S(1)} %get-tuple-element.42.x_ref.c_ref), custom_call_target="tpu_custom_call" | custom-call | flops 536870912 | bytes 2097152 | tf_op jit(solution)/shard_map/gram/pallas_call | solution.py:210
  51.8 3.1 %gram.3.g_ref = bf16[512,512]{1,0:T(8,128)(2,1)S(1)} custom-call(s32[20,32]{1,0:T(8,128)S(1)} %bitcast.7, bf16[512,2048]{1,0:T(8,128)(2,1)S(1)} %get-tuple-element.41.x_ref.v_ref, bf16[512,2048]{1,0:T(8,128)(2,1)S(1)} %get-tuple-element.42.x_ref.c_ref), custom_call_target="tpu_custom_call" | custom-call | flops 536870912 | bytes 2097152 | tf_op jit(solution)/shard_map/gram/pallas_call | solution.py:210
  54.9 4.3 %intra.2 = (bf16[512,2048]{1,0:T(8,128)(2,1)S(1)}, bf16[512,2048]{1,0:T(8,128)(2,1)S(1)}, f32[512,128]{1,0:T(8,128)S(1)}, f32[512,128]{1,0:T(8,128)S(1)}) custom-call(s32[20,32]{1,0:T(8,128)S(1)} %bitcast.8, bf16[512,2048]{1,0:T(8,128)(2,1)S(1)} %get-tuple-element.41.x_ref.v_ref, bf16[512,2048]{1,0:T(8,128)(2,1)S(1)} %get-tuple-element.42.x_ref.c_ref, ...), custom_call_target="tpu_custom_call" | custom-call | flops 1073741824 | bytes 4194304 | tf_op jit(solution)/shard_map/intra/pallas_call | solution.py:290
  59.2 4.2 %intra.3 = (bf16[512,2048]{1,0:T(8,128)(2,1)S(1)}, bf16[512,2048]{1,0:T(8,128)(2,1)S(1)}, f32[512,128]{1,0:T(8,128)S(1)}, f32[512,128]{1,0:T(8,128)S(1)}) custom-call(s32[20,32]{1,0:T(8,128)S(1)} %bitcast.9, bf16[512,2048]{1,0:T(8,128)(2,1)S(1)} %get-tuple-element.41.x_ref.v_ref, ...), custom_call_target="tpu_custom_call", output_to_operand_aliasing={{0}: (6, {}), {1}: (7, {})} | custom-call | flops 1073741824 | bytes 4194304 | tf_op jit(solution)/shard_map/intra/pallas_call | solution.py:290
  63.4 1.2 %near.2.near_ref = f32[2048,128]{1,0:T(8,128)S(1)} custom-call(s32[20,32]{1,0:T(8,128)S(1)} %bitcast.10, s32[1]{0:T(128)S(6)} %copy.16.window_ref, bf16[2048,128]{1,0:T(8,128)(2,1)S(1)} %collective-permute-done.6.p_ref.b_ref, bf16[4,2048,128]{2,1,0:T(8,128)(2,1)S(1)} %bitcast.3), custom_call_target="tpu_custom_call" | custom-call | flops 2621440 | bytes 2097152 | tf_op jit(solution)/shard_map/near/pallas_call | solution.py:322
  64.7 0.9 %slope.2 = (bf16[2048,128]{1,0:T(8,128)(2,1)S(1)}, bf16[2,128,128]{2,1,0:T(8,128)(2,1)S(1)}, bf16[2,128,128]{2,1,0:T(8,128)(2,1)S(1)}, bf16[2,128,128]{2,1,0:T(8,128)(2,1)S(1)}, bf16[2,128,128]{2,1,0:T(8,128)(2,1)S(1)}) custom-call(f32[2048,128]{1,0:T(8,128)S(1)} %near.2.near_ref, bf16[1024,128]{1,0:T(8,128)(2,1)S(1)} %far.2.mine_ref, ...), custom_call_target="tpu_custom_call" | custom-call | flops 268435456 | bytes 2097152 | tf_op jit(solution)/shard_map/slope/pallas_call | solution.py:423
  65.6 1.8 %collective-permute-start.14 = (bf16[2,128,128]{2,1,0:T(8,128)(2,1)S(1)}, bf16[2,128,128]{2,1,0:T(8,128)(2,1)S(1)}, u32[]{:S(2)}, u32[]{:S(2)}) collective-permute-start(bf16[2,128,128]{2,1,0:T(8,128)(2,1)S(1)} %get-tuple-element.66), channel_id=1, source_target_pairs={{0,1},{1,0},{2,3},{3,2},{4,5},{5,4},{6,7},{7,6},{8,9},{9,8},{10,11... | collective-permute-start | bytes 196616 | tf_op jit(solution)/shard_map/ppermute | solution.py:30
  67.4 1.6 %collective-permute-start.15 = (bf16[2,128,128]{2,1,0:T(8,128)(2,1)S(1)}, bf16[2,128,128]{2,1,0:T(8,128)(2,1)S(1)}, u32[]{:S(2)}, u32[]{:S(2)}) collective-permute-start(bf16[2,128,128]{2,1,0:T(8,128)(2,1)S(1)} %get-tuple-element.67), channel_id=1, source_target_pairs={{0,2},{1,3},{2,0},{3,1},{4,6},{5,7},{6,4},{7,5},{8,10},{9,11},{10,... | collective-permute-start | bytes 196616 | tf_op jit(solution)/shard_map/ppermute | solution.py:30
  69.0 1.1 %collective-permute-start.16 = (bf16[2,128,128]{2,1,0:T(8,128)(2,1)S(1)}, bf16[2,128,128]{2,1,0:T(8,128)(2,1)S(1)}, u32[]{:S(2)}, u32[]{:S(2)}) collective-permute-start(bf16[2,128,128]{2,1,0:T(8,128)(2,1)S(1)} %get-tuple-element.68), channel_id=1, source_target_pairs={{0,3},{1,2},{2,1},{3,0},{4,7},{5,6},{6,5},{7,4},{8,11},{9,10},{10,... | collective-permute-start | bytes 196616 | tf_op jit(solution)/shard_map/ppermute | solution.py:30
  70.9 0.9 %slope.3 = (bf16[2048,128]{1,0:T(8,128)(2,1)S(1)}, bf16[2,128,128]{2,1,0:T(8,128)(2,1)S(1)}, bf16[2,128,128]{2,1,0:T(8,128)(2,1)S(1)}, bf16[2,128,128]{2,1,0:T(8,128)(2,1)S(1)}, bf16[2,128,128]{2,1,0:T(8,128)(2,1)S(1)}) custom-call(f32[2048,128]{1,0:T(8,128)S(1)} %near.3.near_ref, bf16[2048,128]{1,0:T(8,128)(2,1)S(1)} %far.3.mine_ref, ...), custom_call_target="tpu_custom_call" | custom-call | flops 268435456 | bytes 2097152 | tf_op jit(solution)/shard_map/slope/pallas_call | solution.py:423
  72.7 2.6 %collective-permute-start.18 = (bf16[2,128,128]{2,1,0:T(8,128)(2,1)S(1)}, bf16[2,128,128]{2,1,0:T(8,128)(2,1)S(1)}, u32[]{:S(2)}, u32[]{:S(2)}) collective-permute-start(bf16[2,128,128]{2,1,0:T(8,128)(2,1)S(1)} %get-tuple-element.73), channel_id=1, source_target_pairs={{0,2},{1,3},{2,0},{3,1},{4,6},{5,7},{6,4},{7,5},{8,10},{9,11},{10,... | collective-permute-start | bytes 196616 | tf_op jit(solution)/shard_map/ppermute | solution.py:30
  75.2 1.1 %collective-permute-start.19 = (bf16[2,128,128]{2,1,0:T(8,128)(2,1)S(1)}, bf16[2,128,128]{2,1,0:T(8,128)(2,1)S(1)}, u32[]{:S(2)}, u32[]{:S(2)}) collective-permute-start(bf16[2,128,128]{2,1,0:T(8,128)(2,1)S(1)} %get-tuple-element.74), channel_id=1, source_target_pairs={{0,3},{1,2},{2,1},{3,0},{4,7},{5,6},{6,5},{7,4},{8,11},{9,10},{10,... | collective-permute-start | bytes 196616 | tf_op jit(solution)/shard_map/ppermute | solution.py:30
  76.3 4.6 %outs.1 = (bf16[512,2048]{1,0:T(8,128)(2,1)}, bf16[512,2048]{1,0:T(8,128)(2,1)}, f32[4,2048,128]{2,1,0:T(8,128)}, f32[128,8,128]{2,1,0:T(8,128)}) custom-call(s32[20,32]{1,0:T(8,128)S(1)} %bitcast.12, s32[1]{0:T(128)S(6)} %copy.16.window_ref, bf16[512,2048]{1,0:T(8,128)(2,1)S(1)} %get-tuple-element.55.mix_ref, ...), custom_call_target="tpu_custom_call" | custom-call | flops 536870912 | bytes 6291456 | tf_op jit(solution)/shard_map/outs/pallas_call | solution.py:496
  81.4 1.0 %gather.1 = f32[128,8,128]{2,1,0:T(8,128)} custom-call(bf16[2,128,128]{2,1,0:T(8,128)(2,1)S(1)} %get-tuple-element.71.refs_0_, bf16[2,128,128]{2,1,0:T(8,128)(2,1)S(1)} %collective-permute-done.17.refs_1_, bf16[2,128,128]{2,1,0:T(8,128)(2,1)S(1)} %collective-permute-done.18.refs_2_, bf16[2,128,128]{2,1,0:T(8,128)(2,1)S(1)} %collective-permute-done.19.refs_3_), custom_call_target="tpu_custom_call" | custom-call | flops 1000000 | bytes 786432 | tf_op jit(solution)/shard_map/gather/pallas_call | solution.py:528
  (31 shorter events, 4.8 us)
Async XLA Ops:
  3.1 5.7 %collective-permute-start.3 = (bf16[2,128,128]{2,1,0:T(8,128)(2,1)S(1)}, bf16[2,128,128]{2,1,0:T(8,128)(2,1)S(1)}, u32[]{:S(2)}, u32[]{:S(2)}) collective-permute-start(bf16[2,128,128]{2,1,0:T(8,128)(2,1)S(1)} %get-tuple-element.49), channel_id=1, source_target_pairs={{0,1},{1,0},{2,3},{3,2},{4,5},{5,4},{6,7},{7,6},{8,9},{9,8},{10,11... | collective-permute-start | bytes 196616 | tf_op jit(solution)/shard_map/ppermute | solution.py:30
  6.2 7.3 %collective-permute-start.4 = (bf16[2,128,128]{2,1,0:T(8,128)(2,1)S(1)}, bf16[2,128,128]{2,1,0:T(8,128)(2,1)S(1)}, u32[]{:S(2)}, u32[]{:S(2)}) collective-permute-start(bf16[2,128,128]{2,1,0:T(8,128)(2,1)S(1)} %get-tuple-element.50), channel_id=1, source_target_pairs={{0,2},{1,3},{2,0},{3,1},{4,6},{5,7},{6,4},{7,5},{8,10},{9,11},{10,... | collective-permute-start | bytes 196616 | tf_op jit(solution)/shard_map/ppermute | solution.py:30
  8.8 6.1 %collective-permute-start.5 = (bf16[2,128,128]{2,1,0:T(8,128)(2,1)S(1)}, bf16[2,128,128]{2,1,0:T(8,128)(2,1)S(1)}, u32[]{:S(2)}, u32[]{:S(2)}) collective-permute-start(bf16[2,128,128]{2,1,0:T(8,128)(2,1)S(1)} %get-tuple-element.51), channel_id=1, source_target_pairs={{0,3},{1,2},{2,1},{3,0},{4,7},{5,6},{6,5},{7,4},{8,11},{9,10},{10,... | collective-permute-start | bytes 196616 | tf_op jit(solution)/shard_map/ppermute | solution.py:30
  15.4 9.2 %collective-permute-start.10 = (bf16[2048,128]{1,0:T(8,128)(2,1)S(1)}, bf16[2048,128]{1,0:T(8,128)(2,1)S(1)}, u32[]{:S(2)}, u32[]{:S(2)}) collective-permute-start(bf16[2048,128]{1,0:T(8,128)(2,1)S(1)} %get-tuple-element.61.a_ref), channel_id=1, source_target_pairs={{0,4},{4,0},{8,12},{12,8},{16,20},{20,16},{24,28},{28,24},{1,5},{5... | collective-permute-start | bytes 1572872 | tf_op jit(solution)/shard_map/ppermute | solution.py:30
  15.5 5.9 %collective-permute-start = (bf16[2,128,128]{2,1,0:T(8,128)(2,1)S(1)}, bf16[2,128,128]{2,1,0:T(8,128)(2,1)S(1)}, u32[]{:S(2)}, u32[]{:S(2)}) collective-permute-start(bf16[2,128,128]{2,1,0:T(8,128)(2,1)S(1)} %get-tuple-element.44), channel_id=1, source_target_pairs={{0,1},{1,0},{2,3},{3,2},{4,5},{5,4},{6,7},{7,6},{8,9},{9,8},{10,11... | collective-permute-start | bytes 196616 | tf_op jit(solution)/shard_map/ppermute | solution.py:30
  15.6 5.8 %collective-permute-start.1 = (bf16[2,128,128]{2,1,0:T(8,128)(2,1)S(1)}, bf16[2,128,128]{2,1,0:T(8,128)(2,1)S(1)}, u32[]{:S(2)}, u32[]{:S(2)}) collective-permute-start(bf16[2,128,128]{2,1,0:T(8,128)(2,1)S(1)} %get-tuple-element.45), channel_id=1, source_target_pairs={{0,2},{1,3},{2,0},{3,1},{4,6},{5,7},{6,4},{7,5},{8,10},{9,11},{10,... | collective-permute-start | bytes 196616 | tf_op jit(solution)/shard_map/ppermute | solution.py:30
  17.9 6.1 %collective-permute-start.2 = (bf16[2,128,128]{2,1,0:T(8,128)(2,1)S(1)}, bf16[2,128,128]{2,1,0:T(8,128)(2,1)S(1)}, u32[]{:S(2)}, u32[]{:S(2)}) collective-permute-start(bf16[2,128,128]{2,1,0:T(8,128)(2,1)S(1)} %get-tuple-element.46), channel_id=1, source_target_pairs={{0,3},{1,2},{2,1},{3,0},{4,7},{5,6},{6,5},{7,4},{8,11},{9,10},{10,... | collective-permute-start | bytes 196616 | tf_op jit(solution)/shard_map/ppermute | solution.py:30
  24.6 16.9 %copy-start.1 = (s32[32,20]{0,1:T(8,128)S(1)}, s32[32,20]{0,1:T(8,128)}, u32[]{:S(2)}) copy-start(s32[32,20]{0,1:T(8,128)} %param.10) | copy-start | bytes 7684
  24.6 2.0 %collective-permute-start.6 = (bf16[2048,128]{1,0:T(8,128)(2,1)S(1)}, bf16[2048,128]{1,0:T(8,128)(2,1)S(1)}, u32[]{:S(2)}, u32[]{:S(2)}) collective-permute-start(bf16[2048,128]{1,0:T(8,128)(2,1)S(1)} %get-tuple-element.56.a_ref), channel_id=1, source_target_pairs={{0,4},{4,0},{8,12},{12,8},{16,20},{20,16},{24,28},{28,24},{1,5},{5... | collective-permute-start | bytes 1572872 | tf_op jit(solution)/shard_map/ppermute | solution.py:30
  24.8 9.2 %collective-permute-start.11 = (bf16[1024,128]{1,0:T(8,128)(2,1)S(1)}, bf16[1024,128]{1,0:T(8,128)(2,1)S(1)}, u32[]{:S(2)}, u32[]{:S(2)}) collective-permute-start(bf16[1024,128]{1,0:T(8,128)(2,1)S(1)} %combine.6.a_ref), channel_id=1, source_target_pairs={{0,8},{4,12},{8,0},{12,4},{16,24},{20,28},{24,16},{28,20},{1,9},{5... | collective-permute-start | bytes 786440 | tf_op jit(solution)/shard_map/ppermute | solution.py:30
  26.6 12.5 %collective-permute-start.7 = (bf16[1024,128]{1,0:T(8,128)(2,1)S(1)}, bf16[1024,128]{1,0:T(8,128)(2,1)S(1)}, u32[]{:S(2)}, u32[]{:S(2)}) collective-permute-start(bf16[1024,128]{1,0:T(8,128)(2,1)S(1)} %combine.4.a_ref), channel_id=1, source_target_pairs={{0,8},{4,12},{8,0},{12,4},{16,24},{20,28},{24,16},{28,20},{1,9},{5... | collective-permute-start | bytes 786440 | tf_op jit(solution)/shard_map/ppermute | solution.py:30
  34.1 7.4 %collective-permute-start.12 = (bf16[1024,128]{1,0:T(8,128)(2,1)S(1)}, bf16[1024,128]{1,0:T(8,128)(2,1)S(1)}, u32[]{:S(2)}, u32[]{:S(2)}) collective-permute-start(bf16[1024,128]{1,0:T(8,128)(2,1)S(1)} %combine.7.refs_2_), channel_id=1, source_target_pairs={{0,16},{4,20},{8,24},{12,28},{16,0},{20,4},{24,8},{28,12},{1,17},{... | collective-permute-start | bytes 786440 | tf_op jit(solution)/shard_map/ppermute | solution.py:30
  39.2 7.9 %collective-permute-start.8 = (bf16[1024,128]{1,0:T(8,128)(2,1)S(1)}, bf16[1024,128]{1,0:T(8,128)(2,1)S(1)}, u32[]{:S(2)}, u32[]{:S(2)}) collective-permute-start(bf16[1024,128]{1,0:T(8,128)(2,1)S(1)} %combine.5), channel_id=1, source_target_pairs={{0,16},{4,20},{8,24},{12,28},{16,0},{20,4},{24,8},{28,12},{1,17},{... | collective-permute-start | bytes 786440 | tf_op jit(solution)/shard_map/ppermute | solution.py:30
  42.4 28.5 %collective-permute-start.13 = (bf16[2048,128]{1,0:T(8,128)(2,1)S(1)}, bf16[2048,128]{1,0:T(8,128)(2,1)S(1)}, u32[]{:S(2)}, u32[]{:S(2)}) collective-permute-start(bf16[2048,128]{1,0:T(8,128)(2,1)S(1)} %far.3.mine_ref), channel_id=1, source_target_pairs={{0,4},{4,0},{8,12},{12,8},{16,20},{20,16},{24,28},{28,24},{1,5},{5... | collective-permute-start | bytes 1572872 | tf_op jit(solution)/shard_map/ppermute | solution.py:30
  48.0 16.7 %collective-permute-start.9 = (bf16[1024,128]{1,0:T(8,128)(2,1)S(1)}, bf16[1024,128]{1,0:T(8,128)(2,1)S(1)}, u32[]{:S(2)}, u32[]{:S(2)}) collective-permute-start(bf16[1024,128]{1,0:T(8,128)(2,1)S(1)} %far.2.mine_ref), channel_id=1, source_target_pairs={{0,4},{4,0},{8,12},{12,8},{16,20},{20,16},{24,28},{28,24},{1,5},{5... | collective-permute-start | bytes 786440 | tf_op jit(solution)/shard_map/ppermute | solution.py:30
  59.1 4.3 %copy-start = (bf16[4,32,64,128]{3,2,1,0:T(8,128)(2,1)S(1)}, bf16[4,32,64,128]{3,2,1,0:T(8,128)(2,1)}, u32[]{:S(2)}) copy-start(bf16[4,32,64,128]{3,2,1,0:T(8,128)(2,1)} %param.12) | copy-start | bytes 6291460
  65.6 9.7 %collective-permute-start.14 = (bf16[2,128,128]{2,1,0:T(8,128)(2,1)S(1)}, bf16[2,128,128]{2,1,0:T(8,128)(2,1)S(1)}, u32[]{:S(2)}, u32[]{:S(2)}) collective-permute-start(bf16[2,128,128]{2,1,0:T(8,128)(2,1)S(1)} %get-tuple-element.66), channel_id=1, source_target_pairs={{0,1},{1,0},{2,3},{3,2},{4,5},{5,4},{6,7},{7,6},{8,9},{9,8},{10,11... | collective-permute-start | bytes 196616 | tf_op jit(solution)/shard_map/ppermute | solution.py:30
  67.4 8.9 %collective-permute-start.15 = (bf16[2,128,128]{2,1,0:T(8,128)(2,1)S(1)}, bf16[2,128,128]{2,1,0:T(8,128)(2,1)S(1)}, u32[]{:S(2)}, u32[]{:S(2)}) collective-permute-start(bf16[2,128,128]{2,1,0:T(8,128)(2,1)S(1)} %get-tuple-element.67), channel_id=1, source_target_pairs={{0,2},{1,3},{2,0},{3,1},{4,6},{5,7},{6,4},{7,5},{8,10},{9,11},{10,... | collective-permute-start | bytes 196616 | tf_op jit(solution)/shard_map/ppermute | solution.py:30
  69.0 7.3 %collective-permute-start.16 = (bf16[2,128,128]{2,1,0:T(8,128)(2,1)S(1)}, bf16[2,128,128]{2,1,0:T(8,128)(2,1)S(1)}, u32[]{:S(2)}, u32[]{:S(2)}) collective-permute-start(bf16[2,128,128]{2,1,0:T(8,128)(2,1)S(1)} %get-tuple-element.68), channel_id=1, source_target_pairs={{0,3},{1,2},{2,1},{3,0},{4,7},{5,6},{6,5},{7,4},{8,11},{9,10},{10,... | collective-permute-start | bytes 196616 | tf_op jit(solution)/shard_map/ppermute | solution.py:30
  71.8 9.1 %collective-permute-start.17 = (bf16[2,128,128]{2,1,0:T(8,128)(2,1)S(1)}, bf16[2,128,128]{2,1,0:T(8,128)(2,1)S(1)}, u32[]{:S(2)}, u32[]{:S(2)}) collective-permute-start(bf16[2,128,128]{2,1,0:T(8,128)(2,1)S(1)} %get-tuple-element.72), channel_id=1, source_target_pairs={{0,1},{1,0},{2,3},{3,2},{4,5},{5,4},{6,7},{7,6},{8,9},{9,8},{10,11... | collective-permute-start | bytes 196616 | tf_op jit(solution)/shard_map/ppermute | solution.py:30
  72.7 8.3 %collective-permute-start.18 = (bf16[2,128,128]{2,1,0:T(8,128)(2,1)S(1)}, bf16[2,128,128]{2,1,0:T(8,128)(2,1)S(1)}, u32[]{:S(2)}, u32[]{:S(2)}) collective-permute-start(bf16[2,128,128]{2,1,0:T(8,128)(2,1)S(1)} %get-tuple-element.73), channel_id=1, source_target_pairs={{0,2},{1,3},{2,0},{3,1},{4,6},{5,7},{6,4},{7,5},{8,10},{9,11},{10,... | collective-permute-start | bytes 196616 | tf_op jit(solution)/shard_map/ppermute | solution.py:30
  75.2 6.2 %collective-permute-start.19 = (bf16[2,128,128]{2,1,0:T(8,128)(2,1)S(1)}, bf16[2,128,128]{2,1,0:T(8,128)(2,1)S(1)}, u32[]{:S(2)}, u32[]{:S(2)}) collective-permute-start(bf16[2,128,128]{2,1,0:T(8,128)(2,1)S(1)} %get-tuple-element.74), channel_id=1, source_target_pairs={{0,3},{1,2},{2,1},{3,0},{4,7},{5,6},{6,5},{7,4},{8,11},{9,10},{10,... | collective-permute-start | bytes 196616 | tf_op jit(solution)/shard_map/ppermute | solution.py:30

commit v2 on v1

--- a/solution.py
+++ b/solution.py
@@ -168,16 +168,12 @@
     tok = v_ref.shape[0]
     blocks = tok // base
     heads = cols // head_dim
-    step = pl.program_id(0)
-    at = group * pl.num_programs(0) + step
-    first_head = at * heads
-    first_col = pl.multiple_of(at * cols, cols)
+    first_head = group * heads
+    first_col = group * cols
     rows_i, cols_i, spread = spread_grid(base)
     is_left, left, right = sides(base, head_dim)
 
-    @pl.when(step == 0)
-    def _():
-        g_sc[...] = jnp.zeros_like(g_sc)
+    g_sc[...] = jnp.zeros_like(g_sc)
 
     for pair in range(heads // 2):
         span = pl.ds(first_col + pair * 2 * head_dim, 2 * head_dim)
@@ -196,12 +192,10 @@
                 scaled = (c_ref[blk(i, base), span].astype(F32) * cw).astype(BF)
                 g_sc[blk(i, base), there] += dot_nt(scaled, v_ref[there, span])
 
-    @pl.when(step == pl.num_programs(0) - 1)
-    def _():
-        for i in range(blocks):
-            here = blk(i, base)
-            g_sc[here, here] = jnp.where(rows_i >= cols_i, g_sc[here, here], 0.0)
-        g_ref[...] = g_sc[...].astype(BF)
+    for i in range(blocks):
+        here = blk(i, base)
+        g_sc[here, here] = jnp.where(rows_i >= cols_i, g_sc[here, here], 0.0)
+    g_ref[...] = g_sc[...].astype(BF)
 
 
 def gram(table, values, cotangent, group, groups, head_dim, cols):
@@ -209,7 +203,6 @@
     base = min(128, tok)
     return pl.pallas_call(
         functools.partial(gram_kernel, base=base, head_dim=head_dim, group=group, cols=cols),
-        grid=(width // groups // cols,),
         in_specs=[SMEM, VMEM, VMEM],
         out_specs=VMEM,
         out_shape=pltpu.VMEM((tok, tok), BF),
@@ -226,30 +219,26 @@
     tok = v_ref.shape[0]
     blocks = tok // base
     heads = cols // head_dim
-    step = pl.program_id(0)
-    at = group * pl.num_programs(0) + step
-    first_head = at * heads
-    first_col = pl.multiple_of(at * cols, cols)
+    first_head = group * heads
+    first_col = group * cols
     rows_i, cols_i, spread = spread_grid(base)
     is_left, left, right = sides(base, head_dim)
 
-    @pl.when(step == 0)
-    def _():
-        for i in range(blocks):
-            here = blk(i, base)
-            q_i, k_i = q_ref[here, :], k_ref[here, :]
-            s_sc[here, :] = jnp.where(rows_i >= cols_i, dot_nt(q_i, k_i), 0.0)
-            st_sc[here, :] = jnp.where(rows_i <= cols_i, dot_nt(k_i, q_i), 0.0)
-            above = blk(0, base, i)
-            rest = blk(i + 1, base, blocks - 1 - i)
-            if i > 0:
-                sb_sc[here, above] = dot_nt(q_i, k_ref[above, :]).astype(BF)
-            if i < blocks - 1:
-                stb_sc[here, rest] = dot_nt(k_i, q_ref[rest, :]).astype(BF)
-            until = blk(0, base, i + 1)
-            below = blk(i, base, blocks - i)
-            qg_ref[here, :] = dot_nn(g_ref[here, until], k_ref[until, :])
-            kg_ref[here, :] = dot_tn(g_ref[below, here], q_ref[below, :])
+    for i in range(blocks):
+        here = blk(i, base)
+        q_i, k_i = q_ref[here, :], k_ref[here, :]
+        s_sc[here, :] = jnp.where(rows_i >= cols_i, dot_nt(q_i, k_i), 0.0)
+        st_sc[here, :] = jnp.where(rows_i <= cols_i, dot_nt(k_i, q_i), 0.0)
+        above = blk(0, base, i)
+        rest = blk(i + 1, base, blocks - 1 - i)
+        if i > 0:
+            sb_sc[here, above] = dot_nt(q_i, k_ref[above, :]).astype(BF)
+        if i < blocks - 1:
+            stb_sc[here, rest] = dot_nt(k_i, q_ref[rest, :]).astype(BF)
+        until = blk(0, base, i + 1)
+        below = blk(i, base, blocks - i)
+        qg_ref[here, :] = dot_nn(g_ref[here, until], k_ref[until, :])
+        kg_ref[here, :] = dot_tn(g_ref[below, here], q_ref[below, :])
 
     mix = [[] for _ in range(blocks)]
     dv = [[] for _ in range(blocks)]
@@ -289,7 +278,6 @@
     base = min(128, tok)
     return pl.pallas_call(
         functools.partial(intra_kernel, base=base, head_dim=head_dim, group=group, cols=cols),
-        grid=(width // groups // cols,),
         in_specs=[SMEM] + [VMEM] * (5 + len(before)),
         out_specs=[VMEM] * 4,
         out_shape=[pltpu.VMEM((tok, width), BF)] * 2 + [pltpu.VMEM((tok, state), F32)] * 2,
@@ -559,7 +547,7 @@
     width = heads_here * head_dim
     half = width // 2
     pieces = head_count if head_count <= 4 and repeats == 1 else 1
-    cols_in = min(4, heads_local) * head_dim
+    cols_in = heads_local * head_dim
     cols = min(8, heads_here // 2) * head_dim
 
     def scattered(own, *sent):

time: 82.5 us -> 80.3 us (0.973)
  Pallas kernels: 29.7 us -> 27.6 us
    pallas_call x2, Pallas kernels: 6.18 us -> 5 us  [gram(): pl.pallas_call(functools.partial(gram_kernel, base=base, head_dim=head_di...]
    pallas_call x2, Pallas kernels: 8.49 us -> 7.32 us  [intra(): pl.pallas_call(functools.partial(intra_kernel, base=base, head_dim=head_d...]
  transfers between devices with their start and end apart: 20 -> 20, of which waited for: 10 -> 10; matrix products, arithmetic and copies ran while one was open for 0% -> 0% of each run, Pallas kernels for 31% -> 29%
where the time goes in v2:
time: 80.3 us; the launch traced here: 80.2 us
  Pallas kernels  27.6 us (34%)
  starting transfers between devices  25.7 us (32%)
  waiting for transfers between devices  25.4 us (32%)
  between operations  1.51 us (2%)
    ppermute x20, starting transfers between devices, swap_with(): lax.ppermute(array, axis, [(i, i ^ mask) for i in range(lax.axis_size(axi...  25.7 us
    ppermute x20, waiting for transfers between devices, swap_with(): lax.ppermute(array, axis, [(i, i ^ mask) for i in range(lax.axis_size(axi...  25.4 us
    pallas_call x2, Pallas kernels, intra(): pl.pallas_call(functools.partial(intra_kernel, base=base, head_dim=head_d...  7.32 us
    pallas_call x2, Pallas kernels, gram(): pl.pallas_call(functools.partial(gram_kernel, base=base, head_dim=head_di...  5 us
    pallas_call x1, Pallas kernels, outs(): pl.pallas_call(functools.partial(outs_kernel, cols=cols, count=count, hea...  4.65 us
    pallas_call x1, Pallas kernels, prep(): pl.pallas_call(functools.partial(prep_kernel, pieces=pieces), in_specs=[H...  2.44 us
    pallas_call x2, Pallas kernels, near(): pl.pallas_call(functools.partial(near_kernel, level=level, gate=gate, hea...  2.06 us
    pallas_call x2, Pallas kernels, slope(): pl.pallas_call(functools.partial(slope_kernel, pieces=pieces), in_specs=[...  1.93 us
  transfers between devices with their start and end apart: 20, of which 10 were waited for; matrix products, arithmetic and copies ran while one was open for 0% of the time, Pallas kernels for 29%

profile of v2, /device:TPU:0, one launch (start us, length us, event | category | flops | bytes accessed | tf_op | source)
XLA Modules:
  0.0 80.2 jit_solution(9650735767796204493)
XLA Ops:
  0.6 2.4 %prep.1 = (bf16[2,128,128]{2,1,0:T(8,128)(2,1)S(1)}, bf16[2,128,128]{2,1,0:T(8,128)(2,1)S(1)}, bf16[2,128,128]{2,1,0:T(8,128)(2,1)S(1)}, bf16[2,128,128]{2,1,0:T...) custom-call(bf16[128,8,128]{2,1,0:T(8,128)(2,1)} %refs_0_.1, ...), custom_call_target="tpu_custom_call" | custom-call | flops 1000000 | bytes 1048576 | tf_op jit(solution)/shard_map/prep/pallas_call | solution.py:85
  3.1 3.1 %collective-permute-start.3 = (bf16[2,128,128]{2,1,0:T(8,128)(2,1)S(1)}, bf16[2,128,128]{2,1,0:T(8,128)(2,1)S(1)}, u32[]{:S(2)}, u32[]{:S(2)}) collective-permute-start(bf16[2,128,128]{2,1,0:T(8,128)(2,1)S(1)} %get-tuple-element.49), channel_id=1, source_target_pairs={{0,1},{1,0},{2,3},{3,2},{4,5},{5,4},{6,7},{7,6},{8,9},{9,8},{10,11... | collective-permute-start | bytes 196616 | tf_op jit(solution)/shard_map/ppermute | solution.py:30
  6.2 2.6 %collective-permute-start.4 = (bf16[2,128,128]{2,1,0:T(8,128)(2,1)S(1)}, bf16[2,128,128]{2,1,0:T(8,128)(2,1)S(1)}, u32[]{:S(2)}, u32[]{:S(2)}) collective-permute-start(bf16[2,128,128]{2,1,0:T(8,128)(2,1)S(1)} %get-tuple-element.50), channel_id=1, source_target_pairs={{0,2},{1,3},{2,0},{3,1},{4,6},{5,7},{6,4},{7,5},{8,10},{9,11},{10,... | collective-permute-start | bytes 196616 | tf_op jit(solution)/shard_map/ppermute | solution.py:30
  8.8 4.7 %collective-permute-done.4.refs_2_ = bf16[2,128,128]{2,1,0:T(8,128)(2,1)S(1)} collective-permute-done((bf16[2,128,128]{2,1,0:T(8,128)(2,1)S(1)}, bf16[2,128,128]{2,1,0:T(8,128)(2,1)S(1)}, u32[]{:S(2)}, u32[]{:S(2)}) %collective-permute-start.4) | collective-permute-done | bytes 65568 | tf_op jit(solution)/shard_map/ppermute | solution.py:30
  13.5 1.4 %collective-permute-done.5.refs_3_ = bf16[2,128,128]{2,1,0:T(8,128)(2,1)S(1)} collective-permute-done((bf16[2,128,128]{2,1,0:T(8,128)(2,1)S(1)}, bf16[2,128,128]{2,1,0:T(8,128)(2,1)S(1)}, u32[]{:S(2)}, u32[]{:S(2)}) %collective-permute-start.5) | collective-permute-done | bytes 65568 | tf_op jit(solution)/shard_map/ppermute | solution.py:30
  15.6 2.3 %collective-permute-start.1 = (bf16[2,128,128]{2,1,0:T(8,128)(2,1)S(1)}, bf16[2,128,128]{2,1,0:T(8,128)(2,1)S(1)}, u32[]{:S(2)}, u32[]{:S(2)}) collective-permute-start(bf16[2,128,128]{2,1,0:T(8,128)(2,1)S(1)} %get-tuple-element.45), channel_id=1, source_target_pairs={{0,2},{1,3},{2,0},{3,1},{4,6},{5,7},{6,4},{7,5},{8,10},{9,11},{10,... | collective-permute-start | bytes 196616 | tf_op jit(solution)/shard_map/ppermute | solution.py:30
  17.9 2.0 %collective-permute-start.2 = (bf16[2,128,128]{2,1,0:T(8,128)(2,1)S(1)}, bf16[2,128,128]{2,1,0:T(8,128)(2,1)S(1)}, u32[]{:S(2)}, u32[]{:S(2)}) collective-permute-start(bf16[2,128,128]{2,1,0:T(8,128)(2,1)S(1)} %get-tuple-element.46), channel_id=1, source_target_pairs={{0,3},{1,2},{2,1},{3,0},{4,7},{5,6},{6,5},{7,4},{8,11},{9,10},{10,... | collective-permute-start | bytes 196616 | tf_op jit(solution)/shard_map/ppermute | solution.py:30
  20.0 1.4 %collective-permute-done.refs_1_ = bf16[2,128,128]{2,1,0:T(8,128)(2,1)S(1)} collective-permute-done((bf16[2,128,128]{2,1,0:T(8,128)(2,1)S(1)}, bf16[2,128,128]{2,1,0:T(8,128)(2,1)S(1)}, u32[]{:S(2)}, u32[]{:S(2)}) %collective-permute-start) | collective-permute-done | bytes 65568 | tf_op jit(solution)/shard_map/ppermute | solution.py:30
  21.4 2.6 %collective-permute-done.2.refs_3_ = bf16[2,128,128]{2,1,0:T(8,128)(2,1)S(1)} collective-permute-done((bf16[2,128,128]{2,1,0:T(8,128)(2,1)S(1)}, bf16[2,128,128]{2,1,0:T(8,128)(2,1)S(1)}, u32[]{:S(2)}, u32[]{:S(2)}) %collective-permute-start.2) | collective-permute-done | bytes 65568 | tf_op jit(solution)/shard_map/ppermute | solution.py:30
  24.8 1.6 %collective-permute-start.11 = (bf16[1024,128]{1,0:T(8,128)(2,1)S(1)}, bf16[1024,128]{1,0:T(8,128)(2,1)S(1)}, u32[]{:S(2)}, u32[]{:S(2)}) collective-permute-start(bf16[1024,128]{1,0:T(8,128)(2,1)S(1)} %combine.6.a_ref), channel_id=1, source_target_pairs={{0,8},{4,12},{8,0},{12,4},{16,24},{20,28},{24,16},{28,20},{1,9},{5... | collective-permute-start | bytes 786440 | tf_op jit(solution)/shard_map/ppermute | solution.py:30
  26.6 1.6 %collective-permute-start.7 = (bf16[1024,128]{1,0:T(8,128)(2,1)S(1)}, bf16[1024,128]{1,0:T(8,128)(2,1)S(1)}, u32[]{:S(2)}, u32[]{:S(2)}) collective-permute-start(bf16[1024,128]{1,0:T(8,128)(2,1)S(1)} %combine.4.a_ref), channel_id=1, source_target_pairs={{0,8},{4,12},{8,0},{12,4},{16,24},{20,28},{24,16},{28,20},{1,9},{5... | collective-permute-start | bytes 786440 | tf_op jit(solution)/shard_map/ppermute | solution.py:30
  28.2 5.8 %collective-permute-done.11.b_ref.refs_0_ = bf16[1024,128]{1,0:T(8,128)(2,1)S(1)} collective-permute-done((bf16[1024,128]{1,0:T(8,128)(2,1)S(1)}, bf16[1024,128]{1,0:T(8,128)(2,1)S(1)}, u32[]{:S(2)}, u32[]{:S(2)}) %collective-permute-start.11) | collective-permute-done | bytes 262176 | tf_op jit(solution)/shard_map/ppermute | solution.py:30
  34.1 1.6 %collective-permute-start.12 = (bf16[1024,128]{1,0:T(8,128)(2,1)S(1)}, bf16[1024,128]{1,0:T(8,128)(2,1)S(1)}, u32[]{:S(2)}, u32[]{:S(2)}) collective-permute-start(bf16[1024,128]{1,0:T(8,128)(2,1)S(1)} %combine.7.refs_2_), channel_id=1, source_target_pairs={{0,16},{4,20},{8,24},{12,28},{16,0},{20,4},{24,8},{28,12},{1,17},{... | collective-permute-start | bytes 786440 | tf_op jit(solution)/shard_map/ppermute | solution.py:30
  35.7 3.5 %collective-permute-done.7.b_ref.refs_0_ = bf16[1024,128]{1,0:T(8,128)(2,1)S(1)} collective-permute-done((bf16[1024,128]{1,0:T(8,128)(2,1)S(1)}, bf16[1024,128]{1,0:T(8,128)(2,1)S(1)}, u32[]{:S(2)}, u32[]{:S(2)}) %collective-permute-start.7) | collective-permute-done | bytes 262176 | tf_op jit(solution)/shard_map/ppermute | solution.py:30
  39.2 1.6 %collective-permute-start.8 = (bf16[1024,128]{1,0:T(8,128)(2,1)S(1)}, bf16[1024,128]{1,0:T(8,128)(2,1)S(1)}, u32[]{:S(2)}, u32[]{:S(2)}) collective-permute-start(bf16[1024,128]{1,0:T(8,128)(2,1)S(1)} %combine.5), channel_id=1, source_target_pairs={{0,16},{4,20},{8,24},{12,28},{16,0},{20,4},{24,8},{28,12},{1,17},{... | collective-permute-start | bytes 786440 | tf_op jit(solution)/shard_map/ppermute | solution.py:30
  41.5 0.9 %far.3.mine_ref = bf16[2048,128]{1,0:T(8,128)(2,1)S(1)} custom-call(s32[20,32]{1,0:T(8,128)S(1)} %bitcast.4, bf16[1024,128]{1,0:T(8,128)(2,1)S(1)} %collective-permute-done.11.b_ref.refs_0_, bf16[1024,128]{1,0:T(8,128)(2,1)S(1)} %collective-permute-done.12.refs_1_, bf16[1024,128]{1,0:T(8,128)(2,1)S(1)} %combine.7.refs_2_), custom_call_target="tpu_custom_call" | custom-call | flops 1310720 | bytes 1048576 | tf_op jit(solution)/shard_map/far/pallas_call | solution.py:369
  42.5 4.6 %collective-permute-done.8.refs_1_ = bf16[1024,128]{1,0:T(8,128)(2,1)S(1)} collective-permute-done((bf16[1024,128]{1,0:T(8,128)(2,1)S(1)}, bf16[1024,128]{1,0:T(8,128)(2,1)S(1)}, u32[]{:S(2)}, u32[]{:S(2)}) %collective-permute-start.8) | collective-permute-done | bytes 262176 | tf_op jit(solution)/shard_map/ppermute | solution.py:30
  47.1 0.9 %far.2.mine_ref = bf16[1024,128]{1,0:T(8,128)(2,1)S(1)} custom-call(s32[20,32]{1,0:T(8,128)S(1)} %bitcast.5, bf16[1024,128]{1,0:T(8,128)(2,1)S(1)} %collective-permute-done.7.b_ref.refs_0_, bf16[1024,128]{1,0:T(8,128)(2,1)S(1)} %collective-permute-done.8.refs_1_), custom_call_target="tpu_custom_call" | custom-call | flops 1310720 | bytes 1048576 | tf_op jit(solution)/shard_map/far/pallas_call | solution.py:369
  48.0 2.5 %gram.2.g_ref = bf16[512,512]{1,0:T(8,128)(2,1)S(1)} custom-call(s32[20,32]{1,0:T(8,128)S(1)} %bitcast.6, bf16[512,2048]{1,0:T(8,128)(2,1)S(1)} %get-tuple-element.41.x_ref.v_ref, bf16[512,2048]{1,0:T(8,128)(2,1)S(1)} %get-tuple-element.42.x_ref.c_ref), custom_call_target="tpu_custom_call" | custom-call | flops 536870912 | bytes 2097152 | tf_op jit(solution)/shard_map/gram/pallas_call | solution.py:204
  51.2 2.5 %gram.3.g_ref = bf16[512,512]{1,0:T(8,128)(2,1)S(1)} custom-call(s32[20,32]{1,0:T(8,128)S(1)} %bitcast.7, bf16[512,2048]{1,0:T(8,128)(2,1)S(1)} %get-tuple-element.41.x_ref.v_ref, bf16[512,2048]{1,0:T(8,128)(2,1)S(1)} %get-tuple-element.42.x_ref.c_ref), custom_call_target="tpu_custom_call" | custom-call | flops 536870912 | bytes 2097152 | tf_op jit(solution)/shard_map/gram/pallas_call | solution.py:204
  53.7 3.7 %intra.2 = (bf16[512,2048]{1,0:T(8,128)(2,1)S(1)}, bf16[512,2048]{1,0:T(8,128)(2,1)S(1)}, f32[512,128]{1,0:T(8,128)S(1)}, f32[512,128]{1,0:T(8,128)S(1)}) custom-call(s32[20,32]{1,0:T(8,128)S(1)} %bitcast.8, bf16[512,2048]{1,0:T(8,128)(2,1)S(1)} %get-tuple-element.41.x_ref.v_ref, bf16[512,2048]{1,0:T(8,128)(2,1)S(1)} %get-tuple-element.42.x_ref.c_ref, ...), custom_call_target="tpu_custom_call" | custom-call | flops 1073741824 | bytes 4194304 | tf_op jit(solution)/shard_map/intra/pallas_call | solution.py:279
  57.4 3.7 %intra.3 = (bf16[512,2048]{1,0:T(8,128)(2,1)S(1)}, bf16[512,2048]{1,0:T(8,128)(2,1)S(1)}, f32[512,128]{1,0:T(8,128)S(1)}, f32[512,128]{1,0:T(8,128)S(1)}) custom-call(s32[20,32]{1,0:T(8,128)S(1)} %bitcast.9, bf16[512,2048]{1,0:T(8,128)(2,1)S(1)} %get-tuple-element.41.x_ref.v_ref, ...), custom_call_target="tpu_custom_call", output_to_operand_aliasing={{0}: (6, {}), {1}: (7, {})} | custom-call | flops 1073741824 | bytes 4194304 | tf_op jit(solution)/shard_map/intra/pallas_call | solution.py:279
  61.1 1.2 %near.2.near_ref = f32[2048,128]{1,0:T(8,128)S(1)} custom-call(s32[20,32]{1,0:T(8,128)S(1)} %bitcast.10, s32[1]{0:T(128)S(6)} %copy.16.window_ref, bf16[2048,128]{1,0:T(8,128)(2,1)S(1)} %collective-permute-done.6.p_ref.b_ref, bf16[4,2048,128]{2,1,0:T(8,128)(2,1)S(1)} %bitcast.3), custom_call_target="tpu_custom_call" | custom-call | flops 2621440 | bytes 2097152 | tf_op jit(solution)/shard_map/near/pallas_call | solution.py:310
  62.3 1.1 %slope.2 = (bf16[2048,128]{1,0:T(8,128)(2,1)S(1)}, bf16[2,128,128]{2,1,0:T(8,128)(2,1)S(1)}, bf16[2,128,128]{2,1,0:T(8,128)(2,1)S(1)}, bf16[2,128,128]{2,1,0:T(8,128)(2,1)S(1)}, bf16[2,128,128]{2,1,0:T(8,128)(2,1)S(1)}) custom-call(f32[2048,128]{1,0:T(8,128)S(1)} %near.2.near_ref, bf16[1024,128]{1,0:T(8,128)(2,1)S(1)} %far.2.mine_ref, ...), custom_call_target="tpu_custom_call" | custom-call | flops 268435456 | bytes 2097152 | tf_op jit(solution)/shard_map/slope/pallas_call | solution.py:411
  63.4 1.8 %collective-permute-start.14 = (bf16[2,128,128]{2,1,0:T(8,128)(2,1)S(1)}, bf16[2,128,128]{2,1,0:T(8,128)(2,1)S(1)}, u32[]{:S(2)}, u32[]{:S(2)}) collective-permute-start(bf16[2,128,128]{2,1,0:T(8,128)(2,1)S(1)} %get-tuple-element.66), channel_id=1, source_target_pairs={{0,1},{1,0},{2,3},{3,2},{4,5},{5,4},{6,7},{7,6},{8,9},{9,8},{10,11... | collective-permute-start | bytes 196616 | tf_op jit(solution)/shard_map/ppermute | solution.py:30
  65.2 1.6 %collective-permute-start.15 = (bf16[2,128,128]{2,1,0:T(8,128)(2,1)S(1)}, bf16[2,128,128]{2,1,0:T(8,128)(2,1)S(1)}, u32[]{:S(2)}, u32[]{:S(2)}) collective-permute-start(bf16[2,128,128]{2,1,0:T(8,128)(2,1)S(1)} %get-tuple-element.67), channel_id=1, source_target_pairs={{0,2},{1,3},{2,0},{3,1},{4,6},{5,7},{6,4},{7,5},{8,10},{9,11},{10,... | collective-permute-start | bytes 196616 | tf_op jit(solution)/shard_map/ppermute | solution.py:30
  66.8 1.1 %collective-permute-start.16 = (bf16[2,128,128]{2,1,0:T(8,128)(2,1)S(1)}, bf16[2,128,128]{2,1,0:T(8,128)(2,1)S(1)}, u32[]{:S(2)}, u32[]{:S(2)}) collective-permute-start(bf16[2,128,128]{2,1,0:T(8,128)(2,1)S(1)} %get-tuple-element.68), channel_id=1, source_target_pairs={{0,3},{1,2},{2,1},{3,0},{4,7},{5,6},{6,5},{7,4},{8,11},{9,10},{10,... | collective-permute-start | bytes 196616 | tf_op jit(solution)/shard_map/ppermute | solution.py:30
  68.8 0.9 %slope.3 = (bf16[2048,128]{1,0:T(8,128)(2,1)S(1)}, bf16[2,128,128]{2,1,0:T(8,128)(2,1)S(1)}, bf16[2,128,128]{2,1,0:T(8,128)(2,1)S(1)}, bf16[2,128,128]{2,1,0:T(8,128)(2,1)S(1)}, bf16[2,128,128]{2,1,0:T(8,128)(2,1)S(1)}) custom-call(f32[2048,128]{1,0:T(8,128)S(1)} %near.3.near_ref, bf16[2048,128]{1,0:T(8,128)(2,1)S(1)} %far.3.mine_ref, ...), custom_call_target="tpu_custom_call" | custom-call | flops 268435456 | bytes 2097152 | tf_op jit(solution)/shard_map/slope/pallas_call | solution.py:411
  70.5 2.6 %collective-permute-start.18 = (bf16[2,128,128]{2,1,0:T(8,128)(2,1)S(1)}, bf16[2,128,128]{2,1,0:T(8,128)(2,1)S(1)}, u32[]{:S(2)}, u32[]{:S(2)}) collective-permute-start(bf16[2,128,128]{2,1,0:T(8,128)(2,1)S(1)} %get-tuple-element.73), channel_id=1, source_target_pairs={{0,2},{1,3},{2,0},{3,1},{4,6},{5,7},{6,4},{7,5},{8,10},{9,11},{10,... | collective-permute-start | bytes 196616 | tf_op jit(solution)/shard_map/ppermute | solution.py:30
  73.0 1.0 %collective-permute-start.19 = (bf16[2,128,128]{2,1,0:T(8,128)(2,1)S(1)}, bf16[2,128,128]{2,1,0:T(8,128)(2,1)S(1)}, u32[]{:S(2)}, u32[]{:S(2)}) collective-permute-start(bf16[2,128,128]{2,1,0:T(8,128)(2,1)S(1)} %get-tuple-element.74), channel_id=1, source_target_pairs={{0,3},{1,2},{2,1},{3,0},{4,7},{5,6},{6,5},{7,4},{8,11},{9,10},{10,... | collective-permute-start | bytes 196616 | tf_op jit(solution)/shard_map/ppermute | solution.py:30
  74.1 4.6 %outs.1 = (bf16[512,2048]{1,0:T(8,128)(2,1)}, bf16[512,2048]{1,0:T(8,128)(2,1)}, f32[4,2048,128]{2,1,0:T(8,128)}, f32[128,8,128]{2,1,0:T(8,128)}) custom-call(s32[20,32]{1,0:T(8,128)S(1)} %bitcast.12, s32[1]{0:T(128)S(6)} %copy.16.window_ref, bf16[512,2048]{1,0:T(8,128)(2,1)S(1)} %get-tuple-element.55.mix_ref, ...), custom_call_target="tpu_custom_call" | custom-call | flops 536870912 | bytes 6291456 | tf_op jit(solution)/shard_map/outs/pallas_call | solution.py:484
  79.2 1.0 %gather.1 = f32[128,8,128]{2,1,0:T(8,128)} custom-call(bf16[2,128,128]{2,1,0:T(8,128)(2,1)S(1)} %get-tuple-element.71.refs_0_, bf16[2,128,128]{2,1,0:T(8,128)(2,1)S(1)} %collective-permute-done.17.refs_1_, bf16[2,128,128]{2,1,0:T(8,128)(2,1)S(1)} %collective-permute-done.18.refs_2_, bf16[2,128,128]{2,1,0:T(8,128)(2,1)S(1)} %collective-permute-done.19.refs_3_), custom_call_target="tpu_custom_call" | custom-call | flops 1000000 | bytes 786432 | tf_op jit(solution)/shard_map/gather/pallas_call | solution.py:516
  (31 shorter events, 4.9 us)
Async XLA Ops:
  3.1 5.7 %collective-permute-start.3 = (bf16[2,128,128]{2,1,0:T(8,128)(2,1)S(1)}, bf16[2,128,128]{2,1,0:T(8,128)(2,1)S(1)}, u32[]{:S(2)}, u32[]{:S(2)}) collective-permute-start(bf16[2,128,128]{2,1,0:T(8,128)(2,1)S(1)} %get-tuple-element.49), channel_id=1, source_target_pairs={{0,1},{1,0},{2,3},{3,2},{4,5},{5,4},{6,7},{7,6},{8,9},{9,8},{10,11... | collective-permute-start | bytes 196616 | tf_op jit(solution)/shard_map/ppermute | solution.py:30
  6.2 7.3 %collective-permute-start.4 = (bf16[2,128,128]{2,1,0:T(8,128)(2,1)S(1)}, bf16[2,128,128]{2,1,0:T(8,128)(2,1)S(1)}, u32[]{:S(2)}, u32[]{:S(2)}) collective-permute-start(bf16[2,128,128]{2,1,0:T(8,128)(2,1)S(1)} %get-tuple-element.50), channel_id=1, source_target_pairs={{0,2},{1,3},{2,0},{3,1},{4,6},{5,7},{6,4},{7,5},{8,10},{9,11},{10,... | collective-permute-start | bytes 196616 | tf_op jit(solution)/shard_map/ppermute | solution.py:30
  8.8 6.1 %collective-permute-start.5 = (bf16[2,128,128]{2,1,0:T(8,128)(2,1)S(1)}, bf16[2,128,128]{2,1,0:T(8,128)(2,1)S(1)}, u32[]{:S(2)}, u32[]{:S(2)}) collective-permute-start(bf16[2,128,128]{2,1,0:T(8,128)(2,1)S(1)} %get-tuple-element.51), channel_id=1, source_target_pairs={{0,3},{1,2},{2,1},{3,0},{4,7},{5,6},{6,5},{7,4},{8,11},{9,10},{10,... | collective-permute-start | bytes 196616 | tf_op jit(solution)/shard_map/ppermute | solution.py:30
  15.4 9.2 %collective-permute-start.10 = (bf16[2048,128]{1,0:T(8,128)(2,1)S(1)}, bf16[2048,128]{1,0:T(8,128)(2,1)S(1)}, u32[]{:S(2)}, u32[]{:S(2)}) collective-permute-start(bf16[2048,128]{1,0:T(8,128)(2,1)S(1)} %get-tuple-element.61.a_ref), channel_id=1, source_target_pairs={{0,4},{4,0},{8,12},{12,8},{16,20},{20,16},{24,28},{28,24},{1,5},{5... | collective-permute-start | bytes 1572872 | tf_op jit(solution)/shard_map/ppermute | solution.py:30
  15.5 5.9 %collective-permute-start = (bf16[2,128,128]{2,1,0:T(8,128)(2,1)S(1)}, bf16[2,128,128]{2,1,0:T(8,128)(2,1)S(1)}, u32[]{:S(2)}, u32[]{:S(2)}) collective-permute-start(bf16[2,128,128]{2,1,0:T(8,128)(2,1)S(1)} %get-tuple-element.44), channel_id=1, source_target_pairs={{0,1},{1,0},{2,3},{3,2},{4,5},{5,4},{6,7},{7,6},{8,9},{9,8},{10,11... | collective-permute-start | bytes 196616 | tf_op jit(solution)/shard_map/ppermute | solution.py:30
  15.6 5.8 %collective-permute-start.1 = (bf16[2,128,128]{2,1,0:T(8,128)(2,1)S(1)}, bf16[2,128,128]{2,1,0:T(8,128)(2,1)S(1)}, u32[]{:S(2)}, u32[]{:S(2)}) collective-permute-start(bf16[2,128,128]{2,1,0:T(8,128)(2,1)S(1)} %get-tuple-element.45), channel_id=1, source_target_pairs={{0,2},{1,3},{2,0},{3,1},{4,6},{5,7},{6,4},{7,5},{8,10},{9,11},{10,... | collective-permute-start | bytes 196616 | tf_op jit(solution)/shard_map/ppermute | solution.py:30
  17.9 6.1 %collective-permute-start.2 = (bf16[2,128,128]{2,1,0:T(8,128)(2,1)S(1)}, bf16[2,128,128]{2,1,0:T(8,128)(2,1)S(1)}, u32[]{:S(2)}, u32[]{:S(2)}) collective-permute-start(bf16[2,128,128]{2,1,0:T(8,128)(2,1)S(1)} %get-tuple-element.46), channel_id=1, source_target_pairs={{0,3},{1,2},{2,1},{3,0},{4,7},{5,6},{6,5},{7,4},{8,11},{9,10},{10,... | collective-permute-start | bytes 196616 | tf_op jit(solution)/shard_map/ppermute | solution.py:30
  24.6 16.9 %copy-start.1 = (s32[32,20]{0,1:T(8,128)S(1)}, s32[32,20]{0,1:T(8,128)}, u32[]{:S(2)}) copy-start(s32[32,20]{0,1:T(8,128)} %param.10) | copy-start | bytes 7684
  24.6 2.0 %collective-permute-start.6 = (bf16[2048,128]{1,0:T(8,128)(2,1)S(1)}, bf16[2048,128]{1,0:T(8,128)(2,1)S(1)}, u32[]{:S(2)}, u32[]{:S(2)}) collective-permute-start(bf16[2048,128]{1,0:T(8,128)(2,1)S(1)} %get-tuple-element.56.a_ref), channel_id=1, source_target_pairs={{0,4},{4,0},{8,12},{12,8},{16,20},{20,16},{24,28},{28,24},{1,5},{5... | collective-permute-start | bytes 1572872 | tf_op jit(solution)/shard_map/ppermute | solution.py:30
  24.8 9.2 %collective-permute-start.11 = (bf16[1024,128]{1,0:T(8,128)(2,1)S(1)}, bf16[1024,128]{1,0:T(8,128)(2,1)S(1)}, u32[]{:S(2)}, u32[]{:S(2)}) collective-permute-start(bf16[1024,128]{1,0:T(8,128)(2,1)S(1)} %combine.6.a_ref), channel_id=1, source_target_pairs={{0,8},{4,12},{8,0},{12,4},{16,24},{20,28},{24,16},{28,20},{1,9},{5... | collective-permute-start | bytes 786440 | tf_op jit(solution)/shard_map/ppermute | solution.py:30
  26.6 12.5 %collective-permute-start.7 = (bf16[1024,128]{1,0:T(8,128)(2,1)S(1)}, bf16[1024,128]{1,0:T(8,128)(2,1)S(1)}, u32[]{:S(2)}, u32[]{:S(2)}) collective-permute-start(bf16[1024,128]{1,0:T(8,128)(2,1)S(1)} %combine.4.a_ref), channel_id=1, source_target_pairs={{0,8},{4,12},{8,0},{12,4},{16,24},{20,28},{24,16},{28,20},{1,9},{5... | collective-permute-start | bytes 786440 | tf_op jit(solution)/shard_map/ppermute | solution.py:30
  34.1 7.4 %collective-permute-start.12 = (bf16[1024,128]{1,0:T(8,128)(2,1)S(1)}, bf16[1024,128]{1,0:T(8,128)(2,1)S(1)}, u32[]{:S(2)}, u32[]{:S(2)}) collective-permute-start(bf16[1024,128]{1,0:T(8,128)(2,1)S(1)} %combine.7.refs_2_), channel_id=1, source_target_pairs={{0,16},{4,20},{8,24},{12,28},{16,0},{20,4},{24,8},{28,12},{1,17},{... | collective-permute-start | bytes 786440 | tf_op jit(solution)/shard_map/ppermute | solution.py:30
  39.2 7.9 %collective-permute-start.8 = (bf16[1024,128]{1,0:T(8,128)(2,1)S(1)}, bf16[1024,128]{1,0:T(8,128)(2,1)S(1)}, u32[]{:S(2)}, u32[]{:S(2)}) collective-permute-start(bf16[1024,128]{1,0:T(8,128)(2,1)S(1)} %combine.5), channel_id=1, source_target_pairs={{0,16},{4,20},{8,24},{12,28},{16,0},{20,4},{24,8},{28,12},{1,17},{... | collective-permute-start | bytes 786440 | tf_op jit(solution)/shard_map/ppermute | solution.py:30
  42.4 26.3 %collective-permute-start.13 = (bf16[2048,128]{1,0:T(8,128)(2,1)S(1)}, bf16[2048,128]{1,0:T(8,128)(2,1)S(1)}, u32[]{:S(2)}, u32[]{:S(2)}) collective-permute-start(bf16[2048,128]{1,0:T(8,128)(2,1)S(1)} %far.3.mine_ref), channel_id=1, source_target_pairs={{0,4},{4,0},{8,12},{12,8},{16,20},{20,16},{24,28},{28,24},{1,5},{5... | collective-permute-start | bytes 1572872 | tf_op jit(solution)/shard_map/ppermute | solution.py:30
  48.0 14.3 %collective-permute-start.9 = (bf16[1024,128]{1,0:T(8,128)(2,1)S(1)}, bf16[1024,128]{1,0:T(8,128)(2,1)S(1)}, u32[]{:S(2)}, u32[]{:S(2)}) collective-permute-start(bf16[1024,128]{1,0:T(8,128)(2,1)S(1)} %far.2.mine_ref), channel_id=1, source_target_pairs={{0,4},{4,0},{8,12},{12,8},{16,20},{20,16},{24,28},{28,24},{1,5},{5... | collective-permute-start | bytes 786440 | tf_op jit(solution)/shard_map/ppermute | solution.py:30
  57.4 3.7 %copy-start = (bf16[4,32,64,128]{3,2,1,0:T(8,128)(2,1)S(1)}, bf16[4,32,64,128]{3,2,1,0:T(8,128)(2,1)}, u32[]{:S(2)}) copy-start(bf16[4,32,64,128]{3,2,1,0:T(8,128)(2,1)} %param.12) | copy-start | bytes 6291460
  63.4 9.6 %collective-permute-start.14 = (bf16[2,128,128]{2,1,0:T(8,128)(2,1)S(1)}, bf16[2,128,128]{2,1,0:T(8,128)(2,1)S(1)}, u32[]{:S(2)}, u32[]{:S(2)}) collective-permute-start(bf16[2,128,128]{2,1,0:T(8,128)(2,1)S(1)} %get-tuple-element.66), channel_id=1, source_target_pairs={{0,1},{1,0},{2,3},{3,2},{4,5},{5,4},{6,7},{7,6},{8,9},{9,8},{10,11... | collective-permute-start | bytes 196616 | tf_op jit(solution)/shard_map/ppermute | solution.py:30
  65.2 8.9 %collective-permute-start.15 = (bf16[2,128,128]{2,1,0:T(8,128)(2,1)S(1)}, bf16[2,128,128]{2,1,0:T(8,128)(2,1)S(1)}, u32[]{:S(2)}, u32[]{:S(2)}) collective-permute-start(bf16[2,128,128]{2,1,0:T(8,128)(2,1)S(1)} %get-tuple-element.67), channel_id=1, source_target_pairs={{0,2},{1,3},{2,0},{3,1},{4,6},{5,7},{6,4},{7,5},{8,10},{9,11},{10,... | collective-permute-start | bytes 196616 | tf_op jit(solution)/shard_map/ppermute | solution.py:30
  66.8 7.3 %collective-permute-start.16 = (bf16[2,128,128]{2,1,0:T(8,128)(2,1)S(1)}, bf16[2,128,128]{2,1,0:T(8,128)(2,1)S(1)}, u32[]{:S(2)}, u32[]{:S(2)}) collective-permute-start(bf16[2,128,128]{2,1,0:T(8,128)(2,1)S(1)} %get-tuple-element.68), channel_id=1, source_target_pairs={{0,3},{1,2},{2,1},{3,0},{4,7},{5,6},{6,5},{7,4},{8,11},{9,10},{10,... | collective-permute-start | bytes 196616 | tf_op jit(solution)/shard_map/ppermute | solution.py:30
  69.6 9.1 %collective-permute-start.17 = (bf16[2,128,128]{2,1,0:T(8,128)(2,1)S(1)}, bf16[2,128,128]{2,1,0:T(8,128)(2,1)S(1)}, u32[]{:S(2)}, u32[]{:S(2)}) collective-permute-start(bf16[2,128,128]{2,1,0:T(8,128)(2,1)S(1)} %get-tuple-element.72), channel_id=1, source_target_pairs={{0,1},{1,0},{2,3},{3,2},{4,5},{5,4},{6,7},{7,6},{8,9},{9,8},{10,11... | collective-permute-start | bytes 196616 | tf_op jit(solution)/shard_map/ppermute | solution.py:30
  70.5 8.3 %collective-permute-start.18 = (bf16[2,128,128]{2,1,0:T(8,128)(2,1)S(1)}, bf16[2,128,128]{2,1,0:T(8,128)(2,1)S(1)}, u32[]{:S(2)}, u32[]{:S(2)}) collective-permute-start(bf16[2,128,128]{2,1,0:T(8,128)(2,1)S(1)} %get-tuple-element.73), channel_id=1, source_target_pairs={{0,2},{1,3},{2,0},{3,1},{4,6},{5,7},{6,4},{7,5},{8,10},{9,11},{10,... | collective-permute-start | bytes 196616 | tf_op jit(solution)/shard_map/ppermute | solution.py:30
  73.0 6.2 %collective-permute-start.19 = (bf16[2,128,128]{2,1,0:T(8,128)(2,1)S(1)}, bf16[2,128,128]{2,1,0:T(8,128)(2,1)S(1)}, u32[]{:S(2)}, u32[]{:S(2)}) collective-permute-start(bf16[2,128,128]{2,1,0:T(8,128)(2,1)S(1)} %get-tuple-element.74), channel_id=1, source_target_pairs={{0,3},{1,2},{2,1},{3,0},{4,7},{5,6},{6,5},{7,4},{8,11},{9,10},{10,... | collective-permute-start | bytes 196616 | tf_op jit(solution)/shard_map/ppermute | solution.py:30
